TPU v7x, 32 devices: a whole 2x2x4 slice. The times are simulated.
32 devices in a mesh: prow: 4 (over x, core), pcol: 8 (over z, y).
Axes of the slice: x: 2, y: 2, z: 4, core: 2. Of those that a mesh axis runs over, the one named last changes fastest.
Arguments:
- slab: float32 [16384, 2048], P('prow', 'pcol'), may hold values from -6 to 6
- panel: float32 [16384, 512], P(('prow', 'pcol')), may hold values from -0.25 to 0.25
- pivots: int32 [512], replicated, may hold values from 0 to 16383, as said below
- inv_lower: float32 [512, 512], replicated, as said below
- inv_upper: float32 [512, 512], replicated, as said below
Outputs:
- updated: float32 [16384, 2048], P('prow', 'pcol')
Inputs may be any that keep to these rules, and one draw needn't show every extreme that they name: `pivots`: 512 distinct row indices. `inv_lower`: unit lower triangular. `inv_upper`: upper triangular with a positive diagonal.
All inputs are finite; a program needn't handle non-finite values.
Results may differ from a plain program's by a relative error of at most 0.000061.
Values sent between devices are 32-bit elements; how exact they have to be, the bound alone decides.
A program may use at most 64 MiB of HBM per device.

v0:
```python
import functools

import jax
import jax.numpy as jnp
from jax import lax
from jax.experimental import pallas as pl
from jax.experimental.pallas import tpu as pltpu
from jax.sharding import PartitionSpec as P

MESH = pl.DeviceIdType.MESH
HIGHEST = lax.Precision.HIGHEST
F32 = jnp.float32
BF16 = jnp.bfloat16


def dot(a, b):
    return jnp.dot(a, b, precision=HIGHEST, preferred_element_type=F32)


def split(a):
    high = a.astype(BF16)
    return high, (a - high.astype(F32)).astype(BF16)


def dot_split(a_high, a_low, b_high, b_low):
    rows = a_high.shape[0]
    both = jnp.dot(
        jnp.concatenate([a_high, a_low], axis=0), b_high, preferred_element_type=F32
    )
    cross = jnp.dot(a_high, b_low, preferred_element_type=F32)
    return both[:rows] + (both[rows:] + cross)


def kernel(
    n_x, n_z, parts,
    slab_ref, panel_ref, pivots_ref, pivot_row_ref, inv_lower_ref, inv_upper_ref,
    out_ref,
    raw, lower, stage, landed, inv_lower, inv_upper, inv_split,
    picked, partner_part, chip_sum, from_x, total, halves, upper,
    load_sem, link_send, link_recv, product_send, product_recv,
    pick_send, pick_recv, x_send, x_recv, half_send, half_recv, raw_peer, peer_send, peer_recv,
):
    slab = out_ref
    prow = lax.axis_index("prow")
    pcol = lax.axis_index("pcol")
    x, core = prow // 2, prow % 2
    z, y = pcol // 2, pcol % 2
    rows = panel_ref.shape[0]
    nb = panel_ref.shape[1]
    piece = rows // parts
    row_count, columns = slab_ref.shape
    half = columns // 2
    first_row = prow * row_count
    partner = {"prow": x * 2 + 1 - core}
    peer = {"pcol": z * 2 + 1 - y}
    left = {"pcol": (z - 1) * 2 + y}
    right = {"pcol": (z + 1) * 2 + y}
    has_left, has_right = z > 0, z < n_z - 1

    loads = [
        pltpu.make_async_copy(slab_ref, slab, load_sem.at[0]),
        pltpu.make_async_copy(panel_ref, raw.at[z], load_sem.at[1]),
        pltpu.make_async_copy(inv_upper_ref, inv_upper, load_sem.at[2]),
        pltpu.make_async_copy(inv_lower_ref, inv_lower, load_sem.at[3]),
    ]
    for load in loads:
        load.start()

    barrier = pltpu.get_barrier_semaphore()
    fixed = [partner, peer] + [
        {"prow": lax.rem(x + o, n_x) * 2 + core} for o in range(1, n_x)
    ]
    for device in fixed:
        pl.semaphore_signal(barrier, inc=1, device_id=device, device_id_type=MESH)
    for exists, device in ((has_left, left), (has_right, right)):
        @pl.when(exists)
        def _():
            pl.semaphore_signal(barrier, inc=1, device_id=device, device_id_type=MESH)
    n_peers = len(fixed) + has_left.astype(jnp.int32) + has_right.astype(jnp.int32)
    pl.semaphore_wait(barrier, n_peers)

    def slot(direction, step, g):
        return (direction * (n_z - 1) + step) * parts + g

    def send(direction, step, g):
        block = z - step if direction == 0 else z + step
        span = pl.ds(g * piece, piece)
        source = panel_ref.at[span] if isinstance(step, int) else raw.at[block, span]
        return pltpu.make_async_remote_copy(
            src_ref=source,
            dst_ref=raw.at[block, span],
            send_sem=link_send.at[slot(direction, step, g)],
            recv_sem=link_recv.at[slot(direction, step, g)],
            device_id=right if direction == 0 else left,
            device_id_type=MESH,
        )

    def sends(direction, step):
        if direction == 0:
            return has_right & (z - step >= 0)
        return has_left & (z + step < n_z)

    def receives(direction, step):
        if direction == 0:
            return z - 1 - step >= 0
        return z + 1 + step < n_z

    def arrived(direction, step, g):
        block = z - 1 - step if direction == 0 else z + 1 + step
        span = pl.ds(g * piece, piece)
        pltpu.make_async_remote_copy(
            src_ref=raw.at[block, span],
            dst_ref=raw.at[block, span],
            send_sem=link_send.at[slot(direction, step, g)],
            recv_sem=link_recv.at[slot(direction, step, g)],
            device_id=left if direction == 0 else right,
            device_id_type=MESH,
        ).wait_recv()
        return block

    for g in range(parts):
        for direction in (0, 1):
            @pl.when(sends(direction, 0))
            def _():
                send(direction, 0, g).start()

    def peer_copy(g):
        span = pl.ds(g * piece, piece)
        return pltpu.make_async_remote_copy(
            src_ref=panel_ref.at[span], dst_ref=raw_peer.at[span],
            send_sem=peer_send.at[g], recv_sem=peer_recv.at[g],
            device_id=peer, device_id_type=MESH,
        )

    for g in range(parts):
        peer_copy(g).start()

    loads[0].wait()

    def pick(k, carry):
        local = pivots_ref[k] - first_row
        inside = (local >= 0) & (local < row_count)
        row = slab[pl.ds(jnp.where(inside, local, 0), 1), :]
        row = jnp.where(inside, row, 0.0)
        picked[0, pl.ds(k, 1), :] = row[:, :half]
        picked[1, pl.ds(k, 1), :] = row[:, half:]
        return carry

    lax.fori_loop(0, nb, pick, 0, unroll=8)

    def remote(source, target, send_sem, recv_sem, device):
        return pltpu.make_async_remote_copy(
            src_ref=source, dst_ref=target, send_sem=send_sem, recv_sem=recv_sem,
            device_id=device, device_id_type=MESH,
        )

    pick_copy = remote(picked.at[1 - core], partner_part, pick_send, pick_recv, partner)
    pick_copy.start()

    def pivot_hits(block, side, g):
        row = first_row + (block * 2 + side) * rows + g * piece
        ids = row + lax.broadcasted_iota(jnp.int32, (piece, nb), 0)
        hits = jnp.where(ids == pivot_row_ref[...], 1.0, 0.0)
        return hits, jnp.max(hits, axis=1, keepdims=True) > 0.0

    def make_lower(block, g):
        span = pl.ds(g * piece, piece)
        high, low = split(raw[block, span, :])
        solved = dot_split(high, low, inv_split[0], inv_split[1])
        hits, is_pivot = pivot_hits(block, y, g)
        high, low = split(jnp.where(is_pivot, -hits, solved))
        lower[0, block, span, :] = high
        lower[1, block, span, :] = low

    pick_copy.wait()
    chip_sum[...] = picked[core] + partner_part[...]
    x_copies = []
    for o in range(1, n_x):
        device = {"prow": lax.rem(x + o, n_x) * 2 + core}
        copy = remote(chip_sum, from_x.at[o - 1], x_send.at[o - 1], x_recv.at[o - 1], device)
        copy.start()
        x_copies.append(copy)

    loads[1].wait()
    loads[2].wait()
    loads[3].wait()
    inv_split[0], inv_split[1] = split(inv_upper[...])
    lax.fori_loop(0, parts, lambda g, c: (make_lower(z, g), c)[1], 0)

    for copy in x_copies:
        copy.wait()
    summed = chip_sum[...]
    for o in range(1, n_x):
        summed = summed + from_x[o - 1]
    total[...] = summed
    halves[core] = dot(inv_lower[...], total[...])
    to_peer = remote(
        halves.at[core], halves.at[2 + core], half_send.at[0], half_recv.at[0], peer
    )
    to_partner = remote(
        halves.at[core], halves.at[core], half_send.at[1], half_recv.at[1], partner
    )
    to_peer.start()
    to_partner.start()

    def pass_on(step, g):
        for direction in (0, 1):
            @pl.when(receives(direction, step))
            def _():
                arrived(direction, step, g)

            @pl.when(receives(direction, step) & sends(direction, step + 1))
            def _():
                send(direction, step + 1, g).start()

    def blocks_of(stage_index):
        step = stage_index - 1
        return (
            (receives(0, step), z - 1 - step),
            (receives(1, step), z + 1 + step),
        )

    def first_stage(g, carry):
        pass_on(jnp.int32(0), g)
        for exists, block in blocks_of(1):
            @pl.when(exists)
            def _():
                make_lower(block, g)
        return carry

    lax.fori_loop(0, parts, first_stage, 0)

    to_partner.wait()
    to_peer.wait()
    onward = remote(
        halves.at[2 + core], halves.at[2 + core], half_send.at[2], half_recv.at[2], partner
    )
    onward.start()
    for i in (0, 1):
        upper[0, :, i * half:(i + 1) * half], upper[1, :, i * half:(i + 1) * half] = (
            split(halves[i])
        )
    onward.wait()
    for i in (2, 3):
        upper[0, :, i * half:(i + 1) * half], upper[1, :, i * half:(i + 1) * half] = (
            split(halves[i])
        )

    def product_copy(block, g):
        span = pl.ds(g * piece, piece)
        index = block * parts + g
        return remote(
            stage.at[block, span], landed.at[block, span],
            product_send.at[index], product_recv.at[index], peer,
        )

    def finish(block, side, g, product, is_pivot):
        start = (block * 2 + side) * rows + g * piece
        span = pl.ds(pl.multiple_of(start, 8), piece)
        slab[span, :] = jnp.where(is_pivot, 0.0, slab[span, :]) - product

    def multiply(block, g):
        span = pl.ds(g * piece, piece)
        products = dot_split(
            lower[0, block, span, :], lower[1, block, span, :], upper[0], upper[1]
        )
        stage[block, span, :] = products[:, columns:]
        product_copy(block, g).start()
        _, is_pivot = pivot_hits(block, y, g)
        finish(block, y, g, products[:, :columns], is_pivot)

    def take(block, g):
        product_copy(block, g).wait_recv()
        _, is_pivot = pivot_hits(block, 1 - y, g)
        span = pl.ds(g * piece, piece)
        finish(block, 1 - y, g, landed[block, span, :], is_pivot)

    def multiply_own(g):
        span = pl.ds(g * piece, piece)
        _, is_pivot = pivot_hits(z, y, g)
        product = dot_split(
            lower[0, z, span, :], lower[1, z, span, :],
            upper[0, :, :columns], upper[1, :, :columns],
        )
        finish(z, y, g, product, is_pivot)

    def take_peer(g):
        peer_copy(g).wait_recv()
        high, low = split(raw_peer[pl.ds(g * piece, piece), :])
        solved = dot_split(high, low, inv_split[0], inv_split[1])
        hits, is_pivot = pivot_hits(z, 1 - y, g)
        high, low = split(jnp.where(is_pivot, -hits, solved))
        product = dot_split(high, low, upper[0, :, :columns], upper[1, :, :columns])
        finish(z, 1 - y, g, product, is_pivot)

    def second_stage(g, carry):
        for exists, block in blocks_of(1):
            @pl.when(exists)
            def _():
                multiply(block, g)
        return carry

    lax.fori_loop(0, parts, second_stage, 0)
    lax.fori_loop(0, parts, lambda g, c: (multiply_own(g), c)[1], 0)

    def late_stage(i, carry):
        stage_index, g = 2 + i // parts, i % parts
        pass_on(stage_index - 1, g)
        for exists, block in blocks_of(stage_index):
            @pl.when(exists)
            def _():
                make_lower(block, g)
                multiply(block, g)

        @pl.when(stage_index == 2)
        def _():
            take_peer(g)

        for exists, block in blocks_of(stage_index - 2):
            @pl.when(exists & (stage_index > 2))
            def _():
                take(block, g)
        return carry

    lax.fori_loop(0, (n_z - 2) * parts, late_stage, 0)

    def last_stage(i, carry):
        stage_index, g = n_z - 2 + i // parts, i % parts

        if n_z == 2:
            @pl.when(stage_index == 0)
            def _():
                take_peer(g)

        for exists, block in blocks_of(stage_index):
            @pl.when(exists & (stage_index > 0))
            def _():
                take(block, g)
        return carry

    lax.fori_loop(0, 2 * parts, last_stage, 0)

    def settle(i, carry):
        block, g = i // parts, i % parts

        @pl.when(block != z)
        def _():
            product_copy(block, g).wait_send()

        @pl.when(block == z)
        def _():
            peer_copy(g).wait_send()
        return carry

    lax.fori_loop(0, n_z * parts, settle, 0)

    def settle_links(i, carry):
        step, g = i // parts, i % parts
        for direction in (0, 1):
            @pl.when(sends(direction, step))
            def _():
                send(direction, step, g).wait_send()
        return carry

    lax.fori_loop(0, (n_z - 1) * parts, settle_links, 0)


def solution(mesh):
    n_prow, n_pcol = mesh.shape["prow"], mesh.shape["pcol"]
    n_x, n_z, parts = n_prow // 2, n_pcol // 2, 4

    def local(slab, panel, pivots, inv_lower, inv_upper):
        (row_count, columns), (rows, nb) = slab.shape, panel.shape
        half = columns // 2
        links = 2 * (n_z - 1) * parts
        hbm = pl.BlockSpec(memory_space=pltpu.HBM)
        dma = pltpu.SemaphoreType.DMA
        flops = 2 * row_count * nb * (nb + columns)
        return pl.pallas_call(
            functools.partial(kernel, n_x, n_z, parts),
            out_shape=pltpu.VMEM(slab.shape, slab.dtype),
            in_specs=[
                hbm,
                hbm,
                pl.BlockSpec(memory_space=pltpu.SMEM),
                pl.BlockSpec(memory_space=pltpu.VMEM),
                hbm,
                hbm,
            ],
            out_specs=pl.BlockSpec(memory_space=pltpu.VMEM),
            scratch_shapes=[
                pltpu.VMEM((n_z, rows, nb), F32),
                pltpu.VMEM((2, n_z, rows, nb), BF16),
                pltpu.VMEM((n_z, rows, columns), F32),
                pltpu.VMEM((n_z, rows, columns), F32),
                pltpu.VMEM((nb, nb), F32),
                pltpu.VMEM((nb, nb), F32),
                pltpu.VMEM((2, nb, nb), BF16),
                pltpu.VMEM((2, nb, half), F32),
                pltpu.VMEM((nb, half), F32),
                pltpu.VMEM((nb, half), F32),
                pltpu.VMEM((max(n_x - 1, 1), nb, half), F32),
                pltpu.VMEM((nb, half), F32),
                pltpu.VMEM((4, nb, half), F32),
                pltpu.VMEM((2, nb, 2 * columns), BF16),
                dma((4,)),
                dma((links,)),
                dma((links,)),
                dma((n_z * parts,)),
                dma((n_z * parts,)),
                dma,
                dma,
                dma((max(n_x - 1, 1),)),
                dma((max(n_x - 1, 1),)),
                dma((3,)),
                dma((3,)),
                pltpu.VMEM((rows, nb), F32),
                dma((parts,)),
                dma((parts,)),
            ],
            compiler_params=pltpu.CompilerParams(
                collective_id=0, has_side_effects=True, vmem_limit_bytes=32 * 2**20
            ),
            cost_estimate=pl.CostEstimate(
                flops=flops, bytes_accessed=8 * slab.size, transcendentals=0
            ),
        )(
            *(pltpu.with_memory_space_constraint(a, pltpu.HBM) for a in (slab, panel)),
            pivots,
            pivots.reshape(1, nb),
            *(pltpu.with_memory_space_constraint(a, pltpu.HBM) for a in (inv_lower, inv_upper)),
        )

    return jax.shard_map(
        local,
        mesh=mesh,
        in_specs=(P("prow", "pcol"), P(("prow", "pcol"), None), P(), P(), P()),
        out_specs=P("prow", "pcol"),
        check_vma=False,
    )
```

profile of v0, /device:TPU:0, one launch (start us, length us, event | category | flops | bytes accessed | tf_op | source)
XLA Modules:
  0.0 82.6 jit_solution(14424780328956516097)
XLA Ops:
  0.0 0.0 copy-start
  0.0 0.7 copy-done
  0.7 79.9 %shard_map.55 = f32[4096,256]{1,0:T(8,128)S(1)} custom-call(f32[4096,256]{1,0:T(8,128)} %slab_ref.1, f32[512,512]{1,0:T(8,128)} %panel_ref.1, s32[512]{0:T(512)S(1)} %copy-done, s32[1,512]{1,0:T(1,128)S(1)} %bitcast.1, f32[512,512]{1,0:T(8,128)} %inv_lower_ref.1, f32[512,512]{1,0:T(8,128)} %inv_upper_ref.1), custom_call_target="tpu_custom_call" | custom-call | flops 3221225472 | bytes 8388608 | tf_op jit(solution)/shard_map/pallas_call | solution.py:379
  80.6 2.0 %copy.7 = f32[4096,256]{1,0:T(8,128)} copy(f32[4096,256]{1,0:T(8,128)S(1)} %shard_map.55) | data formatting | bytes 8388608
Async XLA Ops:
  0.0 0.7 copy-start
where the time goes:
time: 82.8 us; the launch traced here: 82.6 us
  Pallas kernels  79.9 us (96%)
  local copies, waits for them, and re-layouts  2.7 us (3%)
    pallas_call x1, Pallas kernels, local(): pl.pallas_call(functools.partial(kernel, n_x, n_z, parts), out_shape=pltp...  79.9 us
    unnamed x3, local copies, waits for them, and re-layouts  2.7 us

commit v1 on v0

v1 whole, which is shorter than its diff:
```python
import functools

import jax
import jax.numpy as jnp
from jax import lax
from jax.experimental import pallas as pl
from jax.experimental.pallas import tpu as pltpu
from jax.sharding import PartitionSpec as P

MESH = pl.DeviceIdType.MESH
HIGHEST = lax.Precision.HIGHEST
F32 = jnp.float32
BF16 = jnp.bfloat16


def dot(a, b):
    return jnp.dot(a, b, precision=HIGHEST, preferred_element_type=F32)


def split(a):
    high = a.astype(BF16)
    return high, (a - high.astype(F32)).astype(BF16)


def dot_split(a_high, a_low, b_high, b_low):
    rows = a_high.shape[0]
    both = jnp.dot(
        jnp.concatenate([a_high, a_low], axis=0), b_high, preferred_element_type=F32
    )
    cross = jnp.dot(a_high, b_low, preferred_element_type=F32)
    return both[:rows] + (both[rows:] + cross)


def kernel(
    n_x, n_z, parts, chunks, early,
    slab_ref, panel_ref, pivots_ref, pivot_row_ref, inv_lower_ref, inv_upper_ref,
    out_ref,
    raw, raw_peer, lower, lower_own, stage, landed, inv_lower, inv_upper, inv_split,
    picked, partner_part, chip_sum, from_x, total, halves, upper,
    load_sem, link_send, link_recv, product_send, product_recv,
    pick_send, pick_recv, x_send, x_recv, half_send, half_recv, peer_send, peer_recv,
):
    slab = out_ref
    prow = lax.axis_index("prow")
    pcol = lax.axis_index("pcol")
    x, core = prow // 2, prow % 2
    z, y = pcol // 2, pcol % 2
    rows, nb = panel_ref.shape
    piece, chunk = rows // parts, rows // chunks
    row_count, columns = slab_ref.shape
    half = columns // 2
    first_row = prow * row_count
    hops = parts * (n_z - 1) // 2
    partner = {"prow": x * 2 + 1 - core}
    peer = {"pcol": z * 2 + 1 - y}
    right = {"pcol": lax.rem(z + 1, n_z) * 2 + y}
    left = {"pcol": lax.rem(z + n_z - 1, n_z) * 2 + y}
    others = [{"prow": lax.rem(x + o, n_x) * 2 + core} for o in range(1, n_x)]

    panel_load = pltpu.make_async_copy(panel_ref, raw.at[z], load_sem.at[0])
    slab_load = pltpu.make_async_copy(slab_ref, slab, load_sem.at[1])
    upper_load = pltpu.make_async_copy(inv_upper_ref, inv_upper, load_sem.at[2])
    lower_load = pltpu.make_async_copy(inv_lower_ref, inv_lower, load_sem.at[3])
    panel_load.start()

    barrier = pltpu.get_barrier_semaphore()
    neighbours = [partner, peer, right, left] + others
    for device in neighbours:
        pl.semaphore_signal(barrier, inc=1, device_id=device, device_id_type=MESH)
    slab_load.start()
    upper_load.start()
    lower_load.start()
    pl.semaphore_wait(barrier, len(neighbours))

    def remote(source, target, send_sem, recv_sem, device):
        return pltpu.make_async_remote_copy(
            src_ref=source, dst_ref=target, send_sem=send_sem, recv_sem=recv_sem,
            device_id=device, device_id_type=MESH,
        )

    def place(direction, q, away):
        distance = q // parts + away
        turn = n_z - distance if direction == 0 else distance
        block = lax.rem(z + turn, n_z)
        part = q % parts if direction == 0 else parts - 1 - q % parts
        return block, part * piece

    def link(direction, q, away):
        block, start = place(direction, q, away)
        spot = raw.at[block, pl.ds(pl.multiple_of(start, 8), piece)]
        index = direction * hops + q
        return remote(
            spot, spot, link_send.at[index], link_recv.at[index],
            right if direction == 0 else left,
        )

    def peer_copy(g):
        span = pl.ds(g * chunk, chunk)
        return remote(
            raw.at[z, span], raw_peer.at[span], peer_send.at[g], peer_recv.at[g], peer
        )

    panel_load.wait()
    for q in range(min(parts, hops)):
        for direction in (0, 1):
            link(direction, q, 0).start()
    for g in range(chunks - 1):
        peer_copy(g).start()

    slab_load.wait()

    def pick(k, carry):
        local = pivots_ref[k] - first_row
        inside = (local >= 0) & (local < row_count)
        row = slab[pl.ds(jnp.where(inside, local, 0), 1), :]
        row = jnp.where(inside, row, 0.0)
        picked[0, pl.ds(k, 1), :] = row[:, :half]
        picked[1, pl.ds(k, 1), :] = row[:, half:]
        return carry

    lax.fori_loop(0, nb, pick, 0, unroll=8)

    pick_copy = remote(picked.at[1 - core], partner_part, pick_send, pick_recv, partner)
    pick_copy.start()
    upper_load.wait()
    lower_load.wait()
    inv_split[0], inv_split[1] = split(inv_upper[...])
    pick_copy.wait()
    chip_sum[...] = picked[core] + partner_part[...]
    x_copies = [
        remote(chip_sum, from_x.at[i], x_send.at[i], x_recv.at[i], device)
        for i, device in enumerate(others)
    ]
    for copy in x_copies:
        copy.start()

    def pivot_hits(start, count):
        ids = first_row + start + lax.broadcasted_iota(jnp.int32, (count, nb), 0)
        return jnp.where(ids == pivot_row_ref[...], 1.0, 0.0)

    def is_pivot(hits):
        return jnp.max(hits, axis=1, keepdims=True) > 0.0

    def solve(rows_in, hits):
        high, low = split(rows_in)
        solved = dot_split(high, low, inv_split[0], inv_split[1])
        return split(jnp.where(is_pivot(hits), -hits, solved))

    def clear(i, carry):
        start = pl.multiple_of(i * chunk, 8)
        span = pl.ds(start, chunk)
        slab[span, :] = jnp.where(
            is_pivot(pivot_hits(start, chunk)), 0.0, slab[span, :]
        )
        return carry

    lax.fori_loop(0, row_count // chunk, clear, 0)

    def solve_own(g, carry):
        span = pl.ds(pl.multiple_of(g * chunk, 8), chunk)
        hits = pivot_hits((z * 2 + y) * rows + g * chunk, chunk)
        lower_own[0, span, :], lower_own[1, span, :] = solve(raw[z, span, :], hits)
        return carry

    lax.fori_loop(0, chunks, solve_own, 0)

    def prepare(q):
        rows_in, hits = [], []
        for direction in (0, 1):
            link(direction, q, 1).wait_recv()

            @pl.when(q + parts < hops)
            def _():
                link(direction, q + parts, 0).start()

            block, start = place(direction, q, 1)
            rows_in.append(raw[block, pl.ds(pl.multiple_of(start, 8), piece), :])
            hits.append(pivot_hits((block * 2 + y) * rows + start, piece))
        lower[0, q], lower[1, q] = solve(
            jnp.concatenate(rows_in, axis=0), jnp.concatenate(hits, axis=0)
        )

    first, second = min(early[0], hops), min(early[1], hops)
    lax.fori_loop(0, first, lambda q, c: (prepare(q), c)[1], 0)

    for copy in x_copies:
        copy.wait()
    summed = chip_sum[...]
    for o in range(1, n_x):
        summed = summed + from_x[o - 1]
    total[...] = summed
    halves[core] = dot(inv_lower[...], total[...])
    to_peer = remote(
        halves.at[core], halves.at[2 + core], half_send.at[0], half_recv.at[0], peer
    )
    to_partner = remote(
        halves.at[core], halves.at[core], half_send.at[1], half_recv.at[1], partner
    )
    to_peer.start()
    to_partner.start()
    peer_copy(chunks - 1).start()

    lax.fori_loop(first, second, lambda q, c: (prepare(q), c)[1], 0)

    to_peer.wait()
    onward = remote(
        halves.at[2 + core], halves.at[2 + core], half_send.at[2], half_recv.at[2], partner
    )
    onward.start()
    to_partner.wait()

    def split_upper(i):
        span = slice(i * half, (i + 1) * half)
        upper[0, :, span], upper[1, :, span] = split(halves[i])

    split_upper(0)
    split_upper(1)
    onward.wait()
    split_upper(2)
    split_upper(3)

    def product_copy(q):
        return remote(
            stage.at[q], landed.at[q], product_send.at[q], product_recv.at[q], peer
        )

    def subtract(start, count, product):
        span = pl.ds(pl.multiple_of(start, 8), count)
        slab[span, :] = slab[span, :] - product

    def subtract_both(q, side, product):
        for direction in (0, 1):
            block, start = place(direction, q, 1)
            subtract(
                (block * 2 + side) * rows + start, piece,
                product[direction * piece:(direction + 1) * piece],
            )

    def multiply(q):
        products = dot_split(lower[0, q], lower[1, q], upper[0], upper[1])
        stage[q] = products[:, columns:]
        product_copy(q).start()
        subtract_both(q, y, products[:, :columns])

    def take(q, carry):
        product_copy(q).wait_recv()
        subtract_both(q, 1 - y, landed[q])
        return carry

    def multiply_own(g):
        span = pl.ds(pl.multiple_of(g * chunk, 8), chunk)
        product = dot_split(
            lower_own[0, span, :], lower_own[1, span, :],
            upper[0, :, :columns], upper[1, :, :columns],
        )
        subtract((z * 2 + y) * rows + g * chunk, chunk, product)

    def multiply_peer(g):
        peer_copy(g).wait_recv()
        span = pl.ds(pl.multiple_of(g * chunk, 8), chunk)
        start = (z * 2 + 1 - y) * rows + g * chunk
        high, low = solve(raw_peer[span, :], pivot_hits(start, chunk))
        product = dot_split(high, low, upper[0, :, :columns], upper[1, :, :columns])
        subtract(start, chunk, product)

    lax.fori_loop(0, second, lambda q, c: (multiply(q), c)[1], 0)

    def taken(i):
        return jnp.minimum(2 * i, jnp.maximum(second + i - 1, 0))

    def steady(i, carry):
        q = second + i
        prepare(q)
        multiply(q)

        @pl.when(i < chunks)
        def _():
            multiply_own(i)
            multiply_peer(i)

        lax.fori_loop(taken(i), taken(i + 1), take, 0)
        return carry

    steps = hops - second
    lax.fori_loop(0, steps, steady, 0)
    for g in range(min(steps, chunks), chunks):
        multiply_own(g)
        multiply_peer(g)

    def settle(q, carry):
        for direction in (0, 1):
            link(direction, q, 0).wait_send()
        product_copy(q).wait_send()
        return carry

    lax.fori_loop(0, hops - 1, settle, 0)
    for g in range(chunks):
        peer_copy(g).wait_send()
    lax.fori_loop(taken(steps), hops, take, 0)
    lax.fori_loop(hops - 1, hops, settle, 0)


def solution(mesh):
    n_prow, n_pcol = mesh.shape["prow"], mesh.shape["pcol"]
    n_x, n_z, parts, chunks, early = n_prow // 2, n_pcol // 2, 8, 4, (1, 4)

    def local(slab, panel, pivots, inv_lower, inv_upper):
        (row_count, columns), (rows, nb) = slab.shape, panel.shape
        half = columns // 2
        hops = parts * (n_z - 1) // 2
        pair = 2 * rows // parts
        hbm = pl.BlockSpec(memory_space=pltpu.HBM)
        dma = pltpu.SemaphoreType.DMA
        flops = 2 * row_count * nb * (nb + columns)
        return pl.pallas_call(
            functools.partial(kernel, n_x, n_z, parts, chunks, early),
            out_shape=pltpu.VMEM(slab.shape, slab.dtype),
            in_specs=[
                hbm,
                hbm,
                pl.BlockSpec(memory_space=pltpu.SMEM),
                pl.BlockSpec(memory_space=pltpu.VMEM),
                hbm,
                hbm,
            ],
            out_specs=pl.BlockSpec(memory_space=pltpu.VMEM),
            scratch_shapes=[
                pltpu.VMEM((n_z, rows, nb), F32),
                pltpu.VMEM((rows, nb), F32),
                pltpu.VMEM((2, hops, pair, nb), BF16),
                pltpu.VMEM((2, rows, nb), BF16),
                pltpu.VMEM((hops, pair, columns), F32),
                pltpu.VMEM((hops, pair, columns), F32),
                pltpu.VMEM((nb, nb), F32),
                pltpu.VMEM((nb, nb), F32),
                pltpu.VMEM((2, nb, nb), BF16),
                pltpu.VMEM((2, nb, half), F32),
                pltpu.VMEM((nb, half), F32),
                pltpu.VMEM((nb, half), F32),
                pltpu.VMEM((max(n_x - 1, 1), nb, half), F32),
                pltpu.VMEM((nb, half), F32),
                pltpu.VMEM((4, nb, half), F32),
                pltpu.VMEM((2, nb, 2 * columns), BF16),
                dma((4,)),
                dma((2 * hops,)),
                dma((2 * hops,)),
                dma((hops,)),
                dma((hops,)),
                dma,
                dma,
                dma((max(n_x - 1, 1),)),
                dma((max(n_x - 1, 1),)),
                dma((3,)),
                dma((3,)),
                dma((chunks,)),
                dma((chunks,)),
            ],
            compiler_params=pltpu.CompilerParams(
                collective_id=0, has_side_effects=True, vmem_limit_bytes=32 * 2**20
            ),
            cost_estimate=pl.CostEstimate(
                flops=flops, bytes_accessed=8 * slab.size, transcendentals=0
            ),
        )(
            *(pltpu.with_memory_space_constraint(a, pltpu.HBM) for a in (slab, panel)),
            pivots,
            pivots.reshape(1, nb),
            *(pltpu.with_memory_space_constraint(a, pltpu.HBM) for a in (inv_lower, inv_upper)),
        )

    return jax.shard_map(
        local,
        mesh=mesh,
        in_specs=(P("prow", "pcol"), P(("prow", "pcol"), None), P(), P(), P()),
        out_specs=P("prow", "pcol"),
        check_vma=False,
    )
```

time: 82.8 us -> 82.3 us (level)
  no operation moved by 1% of the time
where the time goes in v1:
time: 82.3 us; the launch traced here: 82.1 us
  Pallas kernels  79.4 us (96%)
  local copies, waits for them, and re-layouts  2.7 us (3%)
    pallas_call x1, Pallas kernels, local(): pl.pallas_call(functools.partial(kernel, n_x, n_z, parts, chunks, early),...  79.4 us
    unnamed x3, local copies, waits for them, and re-layouts  2.7 us

profile of v1, /device:TPU:0, one launch (start us, length us, event | category | flops | bytes accessed | tf_op | source)
XLA Modules:
  0.0 82.1 jit_solution(9801444977012388984)
XLA Ops:
  0.0 0.0 copy-start
  0.0 0.7 copy-done
  0.7 79.4 %shard_map.55 = f32[4096,256]{1,0:T(8,128)S(1)} custom-call(f32[4096,256]{1,0:T(8,128)} %slab_ref.1, f32[512,512]{1,0:T(8,128)} %panel_ref.1, s32[512]{0:T(512)S(1)} %copy-done, s32[1,512]{1,0:T(1,128)S(1)} %bitcast.1, f32[512,512]{1,0:T(8,128)} %inv_lower_ref.1, f32[512,512]{1,0:T(8,128)} %inv_upper_ref.1), custom_call_target="tpu_custom_call" | custom-call | flops 3221225472 | bytes 8388608 | tf_op jit(solution)/shard_map/pallas_call | solution.py:315
  80.1 2.0 %copy.7 = f32[4096,256]{1,0:T(8,128)} copy(f32[4096,256]{1,0:T(8,128)S(1)} %shard_map.55) | data formatting | bytes 8388608
Async XLA Ops:
  0.0 0.7 copy-start

commit v2 on v1

v2 whole, which is shorter than its diff:
```python
import functools

import jax
import jax.numpy as jnp
from jax import lax
from jax.experimental import pallas as pl
from jax.experimental.pallas import tpu as pltpu
from jax.sharding import PartitionSpec as P

MESH = pl.DeviceIdType.MESH
HIGHEST = lax.Precision.HIGHEST
F32 = jnp.float32
BF16 = jnp.bfloat16


def dot(a, b):
    return jnp.dot(a, b, precision=HIGHEST, preferred_element_type=F32)


def split(a):
    high = a.astype(BF16)
    return high, (a - high.astype(F32)).astype(BF16)


def dot_split(a_high, a_low, b_high, b_low):
    rows = a_high.shape[0]
    both = jnp.dot(
        jnp.concatenate([a_high, a_low], axis=0), b_high, preferred_element_type=F32
    )
    cross = jnp.dot(a_high, b_low, preferred_element_type=F32)
    return both[:rows] + (both[rows:] + cross)


def kernel(
    n_x, n_z, parts, chunks, ahead, early,
    slab_ref, panel_ref, pivots_ref, pivot_row_ref, inv_lower_ref, inv_upper_ref,
    out_ref,
    raw, raw_peer, lower, stage, landed, inv_lower, inv_upper, inv_split,
    picked, partner_part, chip_sum, from_x, total, halves, upper, pivots, pivot_row,
    load_sem, link_send, link_recv, product_send, product_recv,
    pick_send, pick_recv, x_send, x_recv, half_send, half_recv, peer_send, peer_recv,
):
    slab = out_ref
    prow = lax.axis_index("prow")
    pcol = lax.axis_index("pcol")
    x, core = prow // 2, prow % 2
    z, y = pcol // 2, pcol % 2
    rows, nb = panel_ref.shape
    piece, chunk = rows // parts, rows // chunks
    row_count, columns = slab_ref.shape
    half = columns // 2
    first_row = prow * row_count
    hops = parts * (n_z - 1)
    partner = {"prow": x * 2 + 1 - core}
    peer = {"pcol": z * 2 + 1 - y}
    left = {"pcol": (z - 1) * 2 + y}
    right = {"pcol": (z + 1) * 2 + y}
    has_left, has_right = z > 0, z < n_z - 1
    others = [{"prow": lax.rem(x + o, n_x) * 2 + core} for o in range(1, n_x)]

    barrier = pltpu.get_barrier_semaphore()
    for exists, device in ((has_left, left), (has_right, right)):
        @pl.when(exists)
        def _():
            pl.semaphore_signal(barrier, inc=1, device_id=device, device_id_type=MESH)
    fixed = [peer] + others + [partner]
    for device in fixed:
        pl.semaphore_signal(barrier, inc=1, device_id=device, device_id_type=MESH)

    panel_load = pltpu.make_async_copy(panel_ref, raw.at[z], load_sem.at[0])
    slab_load = pltpu.make_async_copy(slab_ref, slab, load_sem.at[1])
    upper_load = pltpu.make_async_copy(inv_upper_ref, inv_upper, load_sem.at[2])
    lower_load = pltpu.make_async_copy(inv_lower_ref, inv_lower, load_sem.at[3])
    pivot_load = pltpu.make_async_copy(pivots_ref, pivots, load_sem.at[4])
    pivot_row_load = pltpu.make_async_copy(pivot_row_ref, pivot_row, load_sem.at[5])
    for load in (panel_load, pivot_load, slab_load, pivot_row_load, upper_load, lower_load):
        load.start()

    def remote(source, target, send_sem, recv_sem, device):
        return pltpu.make_async_remote_copy(
            src_ref=source, dst_ref=target, send_sem=send_sem, recv_sem=recv_sem,
            device_id=device, device_id_type=MESH,
        )

    def span_of(start, count):
        return pl.ds(pl.multiple_of(start, 8), count)

    def place(direction, q, away):
        distance = q // parts + away
        block = z - distance if direction == 0 else z + distance
        return block, (q % parts) * piece

    def sends(direction, q):
        block, _ = place(direction, q, 0)
        return has_right & (block >= 0) if direction == 0 else has_left & (block < n_z)

    def receives(direction, q):
        block, _ = place(direction, q, 1)
        return block >= 0 if direction == 0 else block < n_z

    def link(direction, q, away):
        block, start = place(direction, q, away)
        spot = raw.at[block, span_of(start, piece)]
        index = direction * hops + q
        return remote(
            spot, spot, link_send.at[index], link_recv.at[index],
            right if direction == 0 else left,
        )

    def peer_copy(g):
        span = span_of(g * chunk, chunk)
        return remote(
            raw.at[z, span], raw_peer.at[span], peer_send.at[g], peer_recv.at[g], peer
        )

    panel_load.wait()
    n_peers = len(fixed) + has_left.astype(jnp.int32) + has_right.astype(jnp.int32)
    pl.semaphore_wait(barrier, n_peers)
    for q in range(parts):
        for direction in (0, 1):
            @pl.when(sends(direction, q))
            def _():
                link(direction, q, 0).start()
    for g in range(ahead[0]):
        peer_copy(g).start()

    pivot_load.wait()
    slab_load.wait()

    def pick(k, carry):
        local = pivots[k] - first_row
        inside = (local >= 0) & (local < row_count)
        row = slab[pl.ds(jnp.where(inside, local, 0), 1), :]
        row = jnp.where(inside, row, 0.0)
        picked[0, pl.ds(k, 1), :] = row[:, :half]
        picked[1, pl.ds(k, 1), :] = row[:, half:]
        return carry

    lax.fori_loop(0, nb, pick, 0, unroll=8)

    pick_copy = remote(picked.at[1 - core], partner_part, pick_send, pick_recv, partner)
    pick_copy.start()
    pivot_row_load.wait()
    upper_load.wait()
    lower_load.wait()
    inv_split[0], inv_split[1] = split(inv_upper[...])
    pick_copy.wait()
    chip_sum[...] = picked[core] + partner_part[...]
    x_copies = [
        remote(chip_sum, from_x.at[i], x_send.at[i], x_recv.at[i], device)
        for i, device in enumerate(others)
    ]
    for copy in x_copies:
        copy.start()

    def pivot_hits(start, count):
        ids = first_row + start + lax.broadcasted_iota(jnp.int32, (count, nb), 0)
        return jnp.where(ids == pivot_row[...], 1.0, 0.0)

    def is_pivot(hits):
        return jnp.max(hits, axis=1, keepdims=True) > 0.0

    def solve(rows_in, hits):
        high, low = split(rows_in)
        solved = dot_split(high, low, inv_split[0], inv_split[1])
        return split(jnp.where(is_pivot(hits), -hits, solved))

    def clear(i, carry):
        start = i * chunk
        span = span_of(start, chunk)
        slab[span, :] = jnp.where(
            is_pivot(pivot_hits(start, chunk)), 0.0, slab[span, :]
        )
        return carry

    lax.fori_loop(0, row_count // chunk, clear, 0)

    def solve_rows(block, start, count):
        span = span_of(start, count)
        hits = pivot_hits((block * 2 + y) * rows + start, count)
        high, low = solve(raw[block, span, :], hits)
        lower[0, block, span, :] = high
        lower[1, block, span, :] = low

    def prepare(q, carry):
        for direction in (0, 1):
            @pl.when(receives(direction, q))
            def _():
                link(direction, q, 1).wait_recv()

            @pl.when(receives(direction, q) & sends(direction, q + parts))
            def _():
                link(direction, q + parts, 0).start()

            @pl.when(receives(direction, q))
            def _():
                solve_rows(*place(direction, q, 1), piece)
        return carry

    first, second = min(early[0], hops), min(early[1], hops)
    lax.fori_loop(0, first, prepare, 0)

    for copy in x_copies:
        copy.wait()
    summed = chip_sum[...]
    for o in range(1, n_x):
        summed = summed + from_x[o - 1]
    total[...] = summed
    halves[core] = dot(inv_lower[...], total[...])
    to_peer = remote(
        halves.at[core], halves.at[2 + core], half_send.at[0], half_recv.at[0], peer
    )
    to_partner = remote(
        halves.at[core], halves.at[core], half_send.at[1], half_recv.at[1], partner
    )
    to_peer.start()
    to_partner.start()
    for g in range(ahead[0], ahead[1]):
        peer_copy(g).start()

    def solve_own(g, carry):
        solve_rows(z, g * chunk, chunk)
        return carry

    lax.fori_loop(0, chunks, solve_own, 0)
    lax.fori_loop(first, second, prepare, 0)

    to_peer.wait()
    onward = remote(
        halves.at[2 + core], halves.at[2 + core], half_send.at[2], half_recv.at[2], partner
    )
    onward.start()
    to_partner.wait()

    def split_upper(i):
        span = slice(i * half, (i + 1) * half)
        upper[0, :, span], upper[1, :, span] = split(halves[i])

    split_upper(0)
    split_upper(1)
    onward.wait()
    split_upper(2)
    split_upper(3)

    def product_copy(direction, q):
        block, start = place(direction, q, 1)
        span = span_of(start, piece)
        index = direction * hops + q
        return remote(
            stage.at[block, span], landed.at[block, span],
            product_send.at[index], product_recv.at[index], peer,
        )

    def subtract(block, side, start, count, product):
        span = span_of((block * 2 + side) * rows + start, count)
        slab[span, :] = slab[span, :] - product

    def multiply(q, carry):
        for direction in (0, 1):
            @pl.when(receives(direction, q))
            def _():
                block, start = place(direction, q, 1)
                span = span_of(start, piece)
                products = dot_split(
                    lower[0, block, span, :], lower[1, block, span, :],
                    upper[0], upper[1],
                )
                stage[block, span, :] = products[:, columns:]
                product_copy(direction, q).start()
                subtract(block, y, start, piece, products[:, :columns])
        return carry

    def take(q, carry):
        for direction in (0, 1):
            @pl.when(receives(direction, q))
            def _():
                block, start = place(direction, q, 1)
                product_copy(direction, q).wait_recv()
                subtract(
                    block, 1 - y, start, piece, landed[block, span_of(start, piece), :]
                )
        return carry

    def multiply_own(g, carry):
        span = span_of(g * chunk, chunk)
        product = dot_split(
            lower[0, z, span, :], lower[1, z, span, :],
            upper[0, :, :columns], upper[1, :, :columns],
        )
        subtract(z, y, g * chunk, chunk, product)
        return carry

    def multiply_peer(g, carry):
        peer_copy(g).wait_recv()
        start = g * chunk
        hits = pivot_hits((z * 2 + 1 - y) * rows + start, chunk)
        high, low = solve(raw_peer[span_of(start, chunk), :], hits)
        product = dot_split(high, low, upper[0, :, :columns], upper[1, :, :columns])
        subtract(z, 1 - y, start, chunk, product)
        return carry

    lax.fori_loop(0, second, multiply, 0)

    steps = hops - second
    middle = steps // 2

    def taken(q):
        return jnp.clip(2 * q - hops + 1, 0, q)

    def reached(i, start):
        return jnp.clip(i - start, 0, chunks)

    def steady(i, carry):
        q = second + i
        prepare(q, 0)
        multiply(q, 0)
        last = ahead[1] + reached(i, 0)

        @pl.when(last < chunks)
        def _():
            peer_copy(last).start()

        lax.fori_loop(reached(i, 0), reached(i + 1, 0), multiply_own, 0)
        lax.fori_loop(reached(i, middle), reached(i + 1, middle), multiply_peer, 0)
        lax.fori_loop(jnp.where(i > 0, taken(q - 1), 0), taken(q), take, 0)
        return carry

    lax.fori_loop(0, steps, steady, 0)
    for g in range(min(ahead[1] + steps, chunks), chunks):
        peer_copy(g).start()
    lax.fori_loop(min(steps, chunks), chunks, multiply_own, 0)
    lax.fori_loop(min(steps - middle, chunks), chunks, multiply_peer, 0)

    def settle(q, carry):
        for direction in (0, 1):
            @pl.when(sends(direction, q))
            def _():
                link(direction, q, 0).wait_send()

            @pl.when(receives(direction, q))
            def _():
                product_copy(direction, q).wait_send()
        return carry

    lax.fori_loop(0, hops - 1, settle, 0)
    for g in range(chunks):
        peer_copy(g).wait_send()
    lax.fori_loop(hops - 1 if steps else 0, hops, take, 0)
    lax.fori_loop(hops - 1, hops, settle, 0)


def solution(mesh):
    n_prow, n_pcol = mesh.shape["prow"], mesh.shape["pcol"]
    n_x, n_z = n_prow // 2, n_pcol // 2
    parts, chunks, ahead, early = 8, 8, (5, 6), (2, 5)

    def local(slab, panel, pivots, inv_lower, inv_upper):
        (row_count, columns), (rows, nb) = slab.shape, panel.shape
        half = columns // 2
        hops = parts * (n_z - 1)
        hbm = pl.BlockSpec(memory_space=pltpu.HBM)
        dma = pltpu.SemaphoreType.DMA
        flops = 2 * row_count * nb * (nb + columns)
        return pl.pallas_call(
            functools.partial(kernel, n_x, n_z, parts, chunks, ahead, early),
            out_shape=pltpu.VMEM(slab.shape, slab.dtype),
            in_specs=[
                hbm,
                hbm,
                hbm,
                hbm,
                hbm,
                hbm,
            ],
            out_specs=pl.BlockSpec(memory_space=pltpu.VMEM),
            scratch_shapes=[
                pltpu.VMEM((n_z, rows, nb), F32),
                pltpu.VMEM((rows, nb), F32),
                pltpu.VMEM((2, n_z, rows, nb), BF16),
                pltpu.VMEM((n_z, rows, columns), F32),
                pltpu.VMEM((n_z, rows, columns), F32),
                pltpu.VMEM((nb, nb), F32),
                pltpu.VMEM((nb, nb), F32),
                pltpu.VMEM((2, nb, nb), BF16),
                pltpu.VMEM((2, nb, half), F32),
                pltpu.VMEM((nb, half), F32),
                pltpu.VMEM((nb, half), F32),
                pltpu.VMEM((max(n_x - 1, 1), nb, half), F32),
                pltpu.VMEM((nb, half), F32),
                pltpu.VMEM((4, nb, half), F32),
                pltpu.VMEM((2, nb, 2 * columns), BF16),
                pltpu.SMEM((nb,), jnp.int32),
                pltpu.VMEM((1, nb), jnp.int32),
                dma((6,)),
                dma((2 * hops,)),
                dma((2 * hops,)),
                dma((2 * hops,)),
                dma((2 * hops,)),
                dma,
                dma,
                dma((max(n_x - 1, 1),)),
                dma((max(n_x - 1, 1),)),
                dma((3,)),
                dma((3,)),
                dma((chunks,)),
                dma((chunks,)),
            ],
            compiler_params=pltpu.CompilerParams(
                collective_id=0, has_side_effects=True, vmem_limit_bytes=32 * 2**20
            ),
            cost_estimate=pl.CostEstimate(
                flops=flops, bytes_accessed=8 * slab.size, transcendentals=0
            ),
        )(
            *(
                pltpu.with_memory_space_constraint(a, pltpu.HBM)
                for a in (slab, panel, pivots, pivots.reshape(1, nb), inv_lower, inv_upper)
            )
        )

    return jax.shard_map(
        local,
        mesh=mesh,
        in_specs=(P("prow", "pcol"), P(("prow", "pcol"), None), P(), P(), P()),
        out_specs=P("prow", "pcol"),
        check_vma=False,
    )
```

time: 82.3 us -> 81 us (0.984)
    unnamed x3 -> x1, local copies, waits for them, and re-layouts: 2.7 us -> 2.02 us
where the time goes in v2:
time: 81 us; the launch traced here: 80.8 us
  Pallas kernels  78.8 us (97%)
  local copies, waits for them, and re-layouts  2.02 us (2%)
    pallas_call x1, Pallas kernels, local(): pl.pallas_call(functools.partial(kernel, n_x, n_z, parts, chunks, ahead,...  78.8 us
    unnamed x1, local copies, waits for them, and re-layouts  2.02 us

profile of v2, /device:TPU:0, one launch (start us, length us, event | category | flops | bytes accessed | tf_op | source)
XLA Modules:
  0.0 80.8 jit_solution(10458410522634830303)
XLA Ops:
  0.0 78.8 %shard_map.55 = f32[4096,256]{1,0:T(8,128)S(1)} custom-call(f32[4096,256]{1,0:T(8,128)} %slab_ref.1, f32[512,512]{1,0:T(8,128)} %panel_ref.1, s32[512]{0:T(512)} %pivots_ref.1, s32[1,512]{1,0:T(1,128)} %bitcast.1, f32[512,512]{1,0:T(8,128)} %inv_lower_ref.1, f32[512,512]{1,0:T(8,128)} %inv_upper_ref.1), custom_call_target="tpu_custom_call" | custom-call | flops 3221225472 | bytes 8388608 | tf_op jit(solution)/shard_map/pallas_call | solution.py:364
  78.8 2.0 %copy.7 = f32[4096,256]{1,0:T(8,128)} copy(f32[4096,256]{1,0:T(8,128)S(1)} %shard_map.55) | data formatting | bytes 8388608

commit v3 on v2

v3 whole, which is shorter than its diff:
```python
import functools

import jax
import jax.numpy as jnp
from jax import lax
from jax.experimental import pallas as pl
from jax.experimental.pallas import tpu as pltpu
from jax.sharding import PartitionSpec as P

MESH = pl.DeviceIdType.MESH
HIGHEST = lax.Precision.HIGHEST
F32 = jnp.float32
BF16 = jnp.bfloat16


def dot(a, b):
    return jnp.dot(a, b, precision=HIGHEST, preferred_element_type=F32)


def split(a):
    high = a.astype(BF16)
    return high, (a - high.astype(F32)).astype(BF16)


def dot_split(a_high, a_low, b_high, b_low):
    rows = a_high.shape[0]
    both = jnp.dot(
        jnp.concatenate([a_high, a_low], axis=0), b_high, preferred_element_type=F32
    )
    cross = jnp.dot(a_high, b_low, preferred_element_type=F32)
    return both[:rows] + (both[rows:] + cross)


def kernel(
    n_x, n_z, early,
    slab_ref, panel_ref, pivots_ref, pivot_row_ref, inv_lower_ref, inv_upper_ref,
    out_ref,
    raw, raw_peer, lower, stage, landed, inv_lower, inv_upper, inv_split,
    picked, partner_part, chip_sum, from_x, total, halves, upper, pivots, pivot_row,
    guest, guest_split, direct, direct_landed,
    load_sem, link_send, link_recv, product_send, product_recv,
    pick_send, pick_recv, x_send, x_recv, half_send, half_recv, peer_send, peer_recv,
    guest_send, guest_recv, direct_send, direct_recv,
):
    slab = out_ref
    prow = lax.axis_index("prow")
    pcol = lax.axis_index("pcol")
    x, core = prow // 2, prow % 2
    z, y = pcol // 2, pcol % 2
    rows, nb = panel_ref.shape
    unit = rows // 8
    pieces = [(0, 2 * unit), (2 * unit, 2 * unit), (4 * unit, 2 * unit)]
    pieces += [(6 * unit, unit), (7 * unit, unit)]
    final = len(pieces) - 1
    peer_pieces = [(0, 2 * unit), (2 * unit, 2 * unit), (4 * unit, unit)]
    peer_pieces += [(5 * unit, unit), (6 * unit, 2 * unit)]
    chunk = 2 * unit
    row_count, columns = slab_ref.shape
    half = columns // 2
    first_row = prow * row_count
    partner = {"prow": x * 2 + 1 - core}
    peer = {"pcol": z * 2 + 1 - y}
    left = {"pcol": (z - 1) * 2 + y}
    right = {"pcol": (z + 1) * 2 + y}
    has_left, has_right = z > 0, z < n_z - 1
    others = [{"prow": lax.rem(x + o, n_x) * 2 + core} for o in range(1, n_x)]

    barrier = pltpu.get_barrier_semaphore()
    for exists, device in ((has_left, left), (has_right, right)):
        @pl.when(exists)
        def _():
            pl.semaphore_signal(barrier, inc=1, device_id=device, device_id_type=MESH)
    fixed = [peer] + others + [partner]
    for device in fixed:
        pl.semaphore_signal(barrier, inc=1, device_id=device, device_id_type=MESH)

    panel_load = pltpu.make_async_copy(panel_ref, raw.at[z], load_sem.at[0])
    slab_load = pltpu.make_async_copy(slab_ref, slab, load_sem.at[1])
    upper_load = pltpu.make_async_copy(inv_upper_ref, inv_upper, load_sem.at[2])
    lower_load = pltpu.make_async_copy(inv_lower_ref, inv_lower, load_sem.at[3])
    pivot_load = pltpu.make_async_copy(pivots_ref, pivots, load_sem.at[4])
    pivot_row_load = pltpu.make_async_copy(pivot_row_ref, pivot_row, load_sem.at[5])
    for load in (panel_load, pivot_load, slab_load, pivot_row_load, upper_load, lower_load):
        load.start()

    def remote(source, target, send_sem, recv_sem, device):
        return pltpu.make_async_remote_copy(
            src_ref=source, dst_ref=target, send_sem=send_sem, recv_sem=recv_sem,
            device_id=device, device_id_type=MESH,
        )

    def span_of(start, count):
        return pl.ds(pl.multiple_of(start, 8), count)

    def block_at(direction, distance):
        return z - distance if direction == 0 else z + distance

    def receives(direction, distance):
        block = block_at(direction, distance)
        return block >= 0 if direction == 0 else block < n_z

    def sends(direction, distance):
        exists = has_right if direction == 0 else has_left
        return exists & receives(direction, distance)

    def guest_of(direction):
        return z == n_z - 1 if direction == 0 else z == 0

    def host_of(direction):
        return z == n_z - 2 if direction == 0 else z == 1

    def comes(direction, distance, g):
        exists = receives(direction, distance)
        if g == final:
            exists &= ~(guest_of(direction) & (distance == 1))
        return exists

    def goes(direction, g):
        exists = sends(direction, 0)
        if g == final:
            exists &= ~host_of(direction)
        return exists

    def link(direction, distance, g):
        block = block_at(direction, distance)
        spot = raw.at[block, pl.ds(*pieces[g])]
        return remote(
            spot, spot, link_send.at[direction * n_z + distance],
            link_recv.at[block * len(pieces) + g], right if direction == 0 else left,
        )

    def peer_copy(i):
        span = pl.ds(*peer_pieces[i])
        return remote(
            raw.at[z, span], raw_peer.at[span], peer_send.at[i], peer_recv.at[i], peer
        )

    panel_load.wait()
    n_peers = len(fixed) + has_left.astype(jnp.int32) + has_right.astype(jnp.int32)
    pl.semaphore_wait(barrier, n_peers)
    for g in range(len(pieces)):
        for direction in (0, 1):
            @pl.when(goes(direction, g))
            def _():
                link(direction, 0, g).start()
    for i in range(3):
        peer_copy(i).start()

    pivot_load.wait()
    slab_load.wait()

    def pick(k, carry):
        local = pivots[k] - first_row
        inside = (local >= 0) & (local < row_count)
        row = slab[pl.ds(jnp.where(inside, local, 0), 1), :]
        row = jnp.where(inside, row, 0.0)
        picked[0, pl.ds(k, 1), :] = row[:, :half]
        picked[1, pl.ds(k, 1), :] = row[:, half:]
        return carry

    lax.fori_loop(0, nb, pick, 0, unroll=8)

    pick_copy = remote(picked.at[1 - core], partner_part, pick_send, pick_recv, partner)
    pick_copy.start()
    pivot_row_load.wait()
    upper_load.wait()
    lower_load.wait()
    inv_split[0], inv_split[1] = split(inv_upper[...])
    pick_copy.wait()
    chip_sum[...] = picked[core] + partner_part[...]
    x_copies = [
        remote(chip_sum, from_x.at[i], x_send.at[i], x_recv.at[i], device)
        for i, device in enumerate(others)
    ]
    for copy in x_copies:
        copy.start()

    def pivot_hits(start, count):
        ids = first_row + start + lax.broadcasted_iota(jnp.int32, (count, nb), 0)
        return jnp.where(ids == pivot_row[...], 1.0, 0.0)

    def is_pivot(hits):
        return jnp.max(hits, axis=1, keepdims=True) > 0.0

    def solve(rows_in, hits):
        high, low = split(rows_in)
        solved = dot_split(high, low, inv_split[0], inv_split[1])
        return split(jnp.where(is_pivot(hits), -hits, solved))

    def clear(i, carry):
        start = i * 2 * chunk
        span = span_of(start, 2 * chunk)
        slab[span, :] = jnp.where(
            is_pivot(pivot_hits(start, 2 * chunk)), 0.0, slab[span, :]
        )
        return carry

    lax.fori_loop(0, row_count // (2 * chunk), clear, 0)

    def solve_rows(block, start, count):
        span = span_of(start, count)
        hits = pivot_hits((block * 2 + y) * rows + start, count)
        high, low = solve(raw[block, span, :], hits)
        lower[0, block, span, :] = high
        lower[1, block, span, :] = low

    def prepare(distance, g):
        for direction in (0, 1):
            arrives = comes(direction, distance, g)

            @pl.when(arrives)
            def _():
                link(direction, distance, g).wait_recv()

            @pl.when(arrives & sends(direction, distance))
            def _():
                link(direction, distance, g).start()

            @pl.when(arrives)
            def _():
                solve_rows(block_at(direction, distance), *pieces[g])

    for g in range(early[0]):
        prepare(1, g)

    for copy in x_copies:
        copy.wait()
    summed = chip_sum[...]
    for o in range(1, n_x):
        summed = summed + from_x[o - 1]
    total[...] = summed
    halves[core] = dot(inv_lower[...], total[...])
    to_peer = remote(
        halves.at[core], halves.at[2 + core], half_send.at[0], half_recv.at[0], peer
    )
    to_partner = remote(
        halves.at[core], halves.at[core], half_send.at[1], half_recv.at[1], partner
    )
    to_peer.start()
    to_partner.start()
    peer_copy(3).start()

    def solve_own(g, carry):
        solve_rows(z, g * chunk, chunk)
        return carry

    lax.fori_loop(0, rows // chunk, solve_own, 0)
    for g in range(early[0], early[1]):
        prepare(1, g)

    to_peer.wait()
    onward = remote(
        halves.at[2 + core], halves.at[2 + core], half_send.at[2], half_recv.at[2], partner
    )
    onward.start()
    to_partner.wait()

    def split_upper(i):
        span = slice(i * half, (i + 1) * half)
        upper[0, :, span], upper[1, :, span] = split(halves[i])

    split_upper(0)
    split_upper(1)
    onward.wait()
    split_upper(2)
    split_upper(3)

    def guest_copy(direction):
        return remote(
            halves.at[0:2], guest.at[direction], guest_send.at[direction],
            guest_recv.at[direction], left if direction == 0 else right,
        )

    def direct_copy(direction):
        return remote(
            direct.at[direction], direct_landed, direct_send.at[direction],
            direct_recv, right if direction == 0 else left,
        )

    for direction in (0, 1):
        @pl.when(guest_of(direction))
        def _():
            guest_copy(direction).start()

    def product_copy(direction, distance, g):
        block = block_at(direction, distance)
        span = pl.ds(*pieces[g])
        return remote(
            stage.at[block, span], landed.at[block, span],
            product_send.at[block], product_recv.at[block * len(pieces) + g], peer,
        )

    def subtract(block, side, start, count, product):
        span = span_of((block * 2 + side) * rows + start, count)
        slab[span, :] = slab[span, :] - product

    def multiply(distance, g):
        start, count = pieces[g]
        span = pl.ds(start, count)
        for direction in (0, 1):
            @pl.when(comes(direction, distance, g))
            def _():
                block = block_at(direction, distance)
                products = dot_split(
                    lower[0, block, span, :], lower[1, block, span, :],
                    upper[0], upper[1],
                )
                stage[block, span, :] = products[:, columns:]
                product_copy(direction, distance, g).start()
                subtract(block, y, start, count, products[:, :columns])

    def take(distance, g):
        start, count = pieces[g]
        for direction in (0, 1):
            @pl.when(comes(direction, distance, g))
            def _():
                block = block_at(direction, distance)
                product_copy(direction, distance, g).wait_recv()
                subtract(
                    block, 1 - y, start, count, landed[block, pl.ds(start, count), :]
                )

    def multiply_own(i, carry):
        span = span_of(i * chunk, chunk)
        product = dot_split(
            lower[0, z, span, :], lower[1, z, span, :],
            upper[0, :, :columns], upper[1, :, :columns],
        )
        subtract(z, y, i * chunk, chunk, product)
        return carry

    def solve_peer(start, count):
        hits = pivot_hits((z * 2 + 1 - y) * rows + start, count)
        return solve(raw_peer[pl.ds(start, count), :], hits)

    def multiply_peer(i):
        for c in ((0,), (1,), (2, 3), (4,))[i]:
            peer_copy(c).wait_recv()
        high, low = solve_peer(i * chunk, chunk)
        product = dot_split(high, low, upper[0, :, :columns], upper[1, :, :columns])
        subtract(z, 1 - y, i * chunk, chunk, product)

    def serve():
        for direction in (0, 1):
            @pl.when(host_of(direction))
            def _():
                guest_copy(direction).wait_recv()
                for i in (0, 1):
                    span = slice(i * half, (i + 1) * half)
                    guest_split[0, :, span], guest_split[1, :, span] = split(
                        guest[direction, i]
                    )
                start, count = pieces[final]
                high, low = solve_peer(start, count)
                direct[direction] = dot_split(
                    jnp.concatenate([lower[0, z, pl.ds(start, count), :], high], axis=0),
                    jnp.concatenate([lower[1, z, pl.ds(start, count), :], low], axis=0),
                    guest_split[0], guest_split[1],
                )
                direct_copy(direction).start()

    for g in range(early[1]):
        multiply(1, g)
    peer_copy(4).start()
    for g in range(early[1], len(pieces)):
        prepare(1, g)
        multiply(1, g)
        lax.fori_loop(2 * (g - early[1]), 2 * (g - early[1]) + 2, multiply_own, 0)

    def step(distance, final_step):
        for g in range(len(pieces)):
            prepare(distance, g)
            multiply(distance, g)
            if isinstance(distance, int) and not final_step and g < 4:
                multiply_peer(g)
            take(distance - 1, g)
            if final_step and g >= 2:
                take(distance, g - 2)

    if n_z <= 3:
        for i in range(4):
            multiply_peer(i)
    if n_z > 3:
        step(2, False)
        lax.fori_loop(3, n_z - 1, lambda d, c: (step(d, False), c)[1], 0)
    serve()
    if n_z > 2:
        step(n_z - 1, True)

    def settle_products(direction, distance):
        block = block_at(direction, distance)

        def wait(count):
            span = pl.ds(0, count)
            remote(
                stage.at[block, span], landed.at[block, span],
                product_send.at[block], product_recv.at[0], peer,
            ).wait_send()

        whole = receives(direction, distance)
        short = guest_of(direction) & (distance == 1)
        pl.when(whole & ~short)(lambda: wait(rows))
        pl.when(whole & short)(lambda: wait(pieces[final][0]))

    def settle_links(direction, distance):
        block = block_at(direction, distance)

        def wait(count):
            spot = raw.at[block, pl.ds(0, count)]
            remote(
                spot, spot, link_send.at[direction * n_z + distance], link_recv.at[0],
                right if direction == 0 else left,
            ).wait_send()

        whole = sends(direction, distance)
        short = host_of(direction) & (distance == 0)
        pl.when(whole & ~short)(lambda: wait(rows))
        pl.when(whole & short)(lambda: wait(pieces[final][0]))

    def settle(distance, carry):
        for direction in (0, 1):
            settle_links(direction, distance)
        return carry

    lax.fori_loop(0, n_z - 1, settle, 0)
    for i in range(len(peer_pieces)):
        peer_copy(i).wait_send()
    for direction in (0, 1):
        @pl.when(guest_of(direction))
        def _():
            guest_copy(direction).wait_send()
    for g in range(final - 1 if n_z > 2 else 0, len(pieces)):
        take(n_z - 1, g)

    def settle_late(distance, carry):
        for direction in (0, 1):
            settle_products(direction, distance)
        return carry

    lax.fori_loop(1, n_z, settle_late, 0)
    for direction in (0, 1):
        @pl.when(host_of(direction))
        def _():
            direct_copy(direction).wait_send()

        @pl.when(guest_of(direction))
        def _():
            direct_copy(direction).wait_recv()
            start, count = pieces[final]
            block = block_at(direction, 1)
            subtract(block, y, start, count, direct_landed[:count])
            subtract(block, 1 - y, start, count, direct_landed[count:])


def solution(mesh):
    n_prow, n_pcol = mesh.shape["prow"], mesh.shape["pcol"]
    n_x, n_z, n_pieces, early = n_prow // 2, n_pcol // 2, 5, (1, 3)

    def local(slab, panel, pivots, inv_lower, inv_upper):
        (row_count, columns), (rows, nb) = slab.shape, panel.shape
        half = columns // 2
        pair = rows // 4
        hbm = pl.BlockSpec(memory_space=pltpu.HBM)
        dma = pltpu.SemaphoreType.DMA
        flops = 2 * row_count * nb * (nb + columns)
        return pl.pallas_call(
            functools.partial(kernel, n_x, n_z, early),
            out_shape=pltpu.VMEM(slab.shape, slab.dtype),
            in_specs=[
                hbm,
                hbm,
                hbm,
                hbm,
                hbm,
                hbm,
            ],
            out_specs=pl.BlockSpec(memory_space=pltpu.VMEM),
            scratch_shapes=[
                pltpu.VMEM((n_z, rows, nb), F32),
                pltpu.VMEM((rows, nb), F32),
                pltpu.VMEM((2, n_z, rows, nb), BF16),
                pltpu.VMEM((n_z, rows, columns), F32),
                pltpu.VMEM((n_z, rows, columns), F32),
                pltpu.VMEM((nb, nb), F32),
                pltpu.VMEM((nb, nb), F32),
                pltpu.VMEM((2, nb, nb), BF16),
                pltpu.VMEM((2, nb, half), F32),
                pltpu.VMEM((nb, half), F32),
                pltpu.VMEM((nb, half), F32),
                pltpu.VMEM((max(n_x - 1, 1), nb, half), F32),
                pltpu.VMEM((nb, half), F32),
                pltpu.VMEM((4, nb, half), F32),
                pltpu.VMEM((2, nb, 2 * columns), BF16),
                pltpu.SMEM((nb,), jnp.int32),
                pltpu.VMEM((1, nb), jnp.int32),
                pltpu.VMEM((2, 2, nb, half), F32),
                pltpu.VMEM((2, nb, columns), BF16),
                pltpu.VMEM((2, pair, columns), F32),
                pltpu.VMEM((pair, columns), F32),
                dma((6,)),
                dma((2 * n_z,)),
                dma((n_pieces * n_z,)),
                dma((n_z,)),
                dma((n_pieces * n_z,)),
                dma,
                dma,
                dma((max(n_x - 1, 1),)),
                dma((max(n_x - 1, 1),)),
                dma((3,)),
                dma((3,)),
                dma((5,)),
                dma((5,)),
                dma((2,)),
                dma((2,)),
                dma((2,)),
                dma,
            ],
            compiler_params=pltpu.CompilerParams(
                collective_id=0, has_side_effects=True, vmem_limit_bytes=32 * 2**20
            ),
            cost_estimate=pl.CostEstimate(
                flops=flops, bytes_accessed=8 * slab.size, transcendentals=0
            ),
        )(
            *(
                pltpu.with_memory_space_constraint(a, pltpu.HBM)
                for a in (slab, panel, pivots, pivots.reshape(1, nb), inv_lower, inv_upper)
            )
        )

    return jax.shard_map(
        local,
        mesh=mesh,
        in_specs=(P("prow", "pcol"), P(("prow", "pcol"), None), P(), P(), P()),
        out_specs=P("prow", "pcol"),
        check_vma=False,
    )
```

time: 81 us -> 78.1 us (0.964)
  Pallas kernels: 78.8 us -> 76 us
    pallas_call x1, Pallas kernels: 78.8 us -> 76 us  [local(): pl.pallas_call(functools.partial(kernel, n_x, n_z, early), out_shape=pltp...]
where the time goes in v3:
time: 78.1 us; the launch traced here: 78 us
  Pallas kernels  76 us (97%)
  local copies, waits for them, and re-layouts  2.02 us (3%)
    pallas_call x1, Pallas kernels, local(): pl.pallas_call(functools.partial(kernel, n_x, n_z, early), out_shape=pltp...  76 us
    unnamed x1, local copies, waits for them, and re-layouts  2.02 us

profile of v3, /device:TPU:0, one launch (start us, length us, event | category | flops | bytes accessed | tf_op | source)
XLA Modules:
  0.0 78.0 jit_solution(16530201475476839165)
XLA Ops:
  0.0 76.0 %shard_map.55 = f32[4096,256]{1,0:T(8,128)S(1)} custom-call(f32[4096,256]{1,0:T(8,128)} %slab_ref.1, f32[512,512]{1,0:T(8,128)} %panel_ref.1, s32[512]{0:T(512)} %pivots_ref.1, s32[1,512]{1,0:T(1,128)} %bitcast.1, f32[512,512]{1,0:T(8,128)} %inv_lower_ref.1, f32[512,512]{1,0:T(8,128)} %inv_upper_ref.1), custom_call_target="tpu_custom_call" | custom-call | flops 3221225472 | bytes 8388608 | tf_op jit(solution)/shard_map/pallas_call | solution.py:466
  76.0 2.0 %copy.7 = f32[4096,256]{1,0:T(8,128)} copy(f32[4096,256]{1,0:T(8,128)S(1)} %shard_map.55) | data formatting | bytes 8388608

commit v4 on v3

--- a/solution.py
+++ b/solution.py
@@ -51,7 +51,9 @@
     unit = rows // 8
     pieces = [(0, 2 * unit), (2 * unit, 2 * unit), (4 * unit, 2 * unit)]
     pieces += [(6 * unit, unit), (7 * unit, unit)]
-    final = len(pieces) - 1
+    late = (3, 4)
+    late_start = pieces[late[0]][0]
+    late_span = pl.ds(late_start, rows - late_start)
     peer_pieces = [(0, 2 * unit), (2 * unit, 2 * unit), (4 * unit, unit)]
     peer_pieces += [(5 * unit, unit), (6 * unit, 2 * unit)]
     chunk = 2 * unit
@@ -111,13 +113,13 @@
 
     def comes(direction, distance, g):
         exists = receives(direction, distance)
-        if g == final:
+        if g in late:
             exists &= ~(guest_of(direction) & (distance == 1))
         return exists
 
     def goes(direction, g):
         exists = sends(direction, 0)
-        if g == final:
+        if g in late:
             exists &= ~host_of(direction)
         return exists
 
@@ -350,11 +352,10 @@
                     guest_split[0, :, span], guest_split[1, :, span] = split(
                         guest[direction, i]
                     )
-                start, count = pieces[final]
-                high, low = solve_peer(start, count)
+                high, low = solve_peer(late_start, rows - late_start)
                 direct[direction] = dot_split(
-                    jnp.concatenate([lower[0, z, pl.ds(start, count), :], high], axis=0),
-                    jnp.concatenate([lower[1, z, pl.ds(start, count), :], low], axis=0),
+                    jnp.concatenate([lower[0, z, late_span, :], high], axis=0),
+                    jnp.concatenate([lower[1, z, late_span, :], low], axis=0),
                     guest_split[0], guest_split[1],
                 )
                 direct_copy(direction).start()
@@ -400,7 +401,7 @@
         whole = receives(direction, distance)
         short = guest_of(direction) & (distance == 1)
         pl.when(whole & ~short)(lambda: wait(rows))
-        pl.when(whole & short)(lambda: wait(pieces[final][0]))
+        pl.when(whole & short)(lambda: wait(late_start))
 
     def settle_links(direction, distance):
         block = block_at(direction, distance)
@@ -415,7 +416,7 @@
         whole = sends(direction, distance)
         short = host_of(direction) & (distance == 0)
         pl.when(whole & ~short)(lambda: wait(rows))
-        pl.when(whole & short)(lambda: wait(pieces[final][0]))
+        pl.when(whole & short)(lambda: wait(late_start))
 
     def settle(distance, carry):
         for direction in (0, 1):
@@ -429,7 +430,7 @@
         @pl.when(guest_of(direction))
         def _():
             guest_copy(direction).wait_send()
-    for g in range(final - 1 if n_z > 2 else 0, len(pieces)):
+    for g in range(3 if n_z > 2 else 0, len(pieces)):
         take(n_z - 1, g)
 
     def settle_late(distance, carry):
@@ -446,10 +447,10 @@
         @pl.when(guest_of(direction))
         def _():
             direct_copy(direction).wait_recv()
-            start, count = pieces[final]
+            count = rows - late_start
             block = block_at(direction, 1)
-            subtract(block, y, start, count, direct_landed[:count])
-            subtract(block, 1 - y, start, count, direct_landed[count:])
+            subtract(block, y, late_start, count, direct_landed[:count])
+            subtract(block, 1 - y, late_start, count, direct_landed[count:])
 
 
 def solution(mesh):
@@ -459,7 +460,7 @@
     def local(slab, panel, pivots, inv_lower, inv_upper):
         (row_count, columns), (rows, nb) = slab.shape, panel.shape
         half = columns // 2
-        pair = rows // 4
+        pair = rows // 2
         hbm = pl.BlockSpec(memory_space=pltpu.HBM)
         dma = pltpu.SemaphoreType.DMA
         flops = 2 * row_count * nb * (nb + columns)

time: 78.1 us -> 75.4 us (0.965)
  Pallas kernels: 76 us -> 73.2 us
    pallas_call x1, Pallas kernels: 76 us -> 73.2 us  [local(): pl.pallas_call(functools.partial(kernel, n_x, n_z, early), out_shape=pltp...]
where the time goes in v4:
time: 75.4 us; the launch traced here: 75.3 us
  Pallas kernels  73.2 us (97%)
  local copies, waits for them, and re-layouts  2.02 us (3%)
    pallas_call x1, Pallas kernels, local(): pl.pallas_call(functools.partial(kernel, n_x, n_z, early), out_shape=pltp...  73.2 us
    unnamed x1, local copies, waits for them, and re-layouts  2.02 us

profile of v4, /device:TPU:0, one launch (start us, length us, event | category | flops | bytes accessed | tf_op | source)
XLA Modules:
  0.0 75.3 jit_solution(10236739540053589385)
XLA Ops:
  0.0 73.2 %shard_map.55 = f32[4096,256]{1,0:T(8,128)S(1)} custom-call(f32[4096,256]{1,0:T(8,128)} %slab_ref.1, f32[512,512]{1,0:T(8,128)} %panel_ref.1, s32[512]{0:T(512)} %pivots_ref.1, s32[1,512]{1,0:T(1,128)} %bitcast.1, f32[512,512]{1,0:T(8,128)} %inv_lower_ref.1, f32[512,512]{1,0:T(8,128)} %inv_upper_ref.1), custom_call_target="tpu_custom_call" | custom-call | flops 3221225472 | bytes 8388608 | tf_op jit(solution)/shard_map/pallas_call | solution.py:467
  73.2 2.0 %copy.7 = f32[4096,256]{1,0:T(8,128)} copy(f32[4096,256]{1,0:T(8,128)S(1)} %shard_map.55) | data formatting | bytes 8388608

commit v5 on v4

--- a/solution.py
+++ b/solution.py
@@ -128,28 +128,35 @@
         spot = raw.at[block, pl.ds(*pieces[g])]
         return remote(
             spot, spot, link_send.at[direction * n_z + distance],
-            link_recv.at[block * len(pieces) + g], right if direction == 0 else left,
+            link_recv.at[(block - direction) * len(pieces) + g],
+            right if direction == 0 else left,
         )
 
     def peer_copy(i):
         span = pl.ds(*peer_pieces[i])
         return remote(
-            raw.at[z, span], raw_peer.at[span], peer_send.at[i], peer_recv.at[i], peer
+            raw.at[z, span], raw_peer.at[span], peer_send, peer_recv.at[i], peer
         )
 
     panel_load.wait()
     n_peers = len(fixed) + has_left.astype(jnp.int32) + has_right.astype(jnp.int32)
     pl.semaphore_wait(barrier, n_peers)
-    for g in range(len(pieces)):
-        for direction in (0, 1):
-            @pl.when(goes(direction, g))
-            def _():
-                link(direction, 0, g).start()
+    def start_links():
+        for loaded in (True, False):
+            for direction in (0, 1):
+                near = (2 * z < n_z) if direction == 1 else (2 * z >= n_z)
+                for g in range(len(pieces)):
+                    @pl.when(goes(direction, g) & (near if loaded else ~near))
+                    def _():
+                        link(direction, 0, g).start()
+
+    pl.when(core == 0)(start_links)
     for i in range(3):
         peer_copy(i).start()
 
     pivot_load.wait()
     slab_load.wait()
+    pl.when(core != 0)(start_links)
 
     def pick(k, carry):
         local = pivots[k] - first_row
@@ -289,7 +296,8 @@
         span = pl.ds(*pieces[g])
         return remote(
             stage.at[block, span], landed.at[block, span],
-            product_send.at[block], product_recv.at[block * len(pieces) + g], peer,
+            product_send.at[block - direction],
+            product_recv.at[(block - direction) * len(pieces) + g], peer,
         )
 
     def subtract(block, side, start, count, product):
@@ -395,7 +403,7 @@
             span = pl.ds(0, count)
             remote(
                 stage.at[block, span], landed.at[block, span],
-                product_send.at[block], product_recv.at[0], peer,
+                product_send.at[block - direction], product_recv.at[0], peer,
             ).wait_send()
 
         whole = receives(direction, distance)
@@ -424,8 +432,7 @@
         return carry
 
     lax.fori_loop(0, n_z - 1, settle, 0)
-    for i in range(len(peer_pieces)):
-        peer_copy(i).wait_send()
+    remote(raw.at[z], raw_peer, peer_send, peer_recv.at[0], peer).wait_send()
     for direction in (0, 1):
         @pl.when(guest_of(direction))
         def _():
@@ -500,16 +507,16 @@
                 pltpu.VMEM((pair, columns), F32),
                 dma((6,)),
                 dma((2 * n_z,)),
-                dma((n_pieces * n_z,)),
-                dma((n_z,)),
-                dma((n_pieces * n_z,)),
+                dma((n_pieces * (n_z - 1),)),
+                dma((n_z - 1,)),
+                dma((n_pieces * (n_z - 1),)),
                 dma,
                 dma,
                 dma((max(n_x - 1, 1),)),
                 dma((max(n_x - 1, 1),)),
                 dma((3,)),
                 dma((3,)),
-                dma((5,)),
+                dma,
                 dma((5,)),
                 dma((2,)),
                 dma((2,)),

time: 75.4 us -> 76.3 us (1.012)
  Pallas kernels: 73.2 us -> 74.1 us
    pallas_call x1, Pallas kernels: 73.2 us -> 74.1 us  [local(): pl.pallas_call(functools.partial(kernel, n_x, n_z, early), out_shape=pltp...]
where the time goes in v5:
time: 76.3 us; the launch traced here: 76.2 us
  Pallas kernels  74.1 us (97%)
  local copies, waits for them, and re-layouts  2.02 us (3%)
    pallas_call x1, Pallas kernels, local(): pl.pallas_call(functools.partial(kernel, n_x, n_z, early), out_shape=pltp...  74.1 us
    unnamed x1, local copies, waits for them, and re-layouts  2.02 us

profile of v5, /device:TPU:0, one launch (start us, length us, event | category | flops | bytes accessed | tf_op | source)
XLA Modules:
  0.0 76.2 jit_solution(16118639238184016060)
XLA Ops:
  0.0 74.1 %shard_map.55 = f32[4096,256]{1,0:T(8,128)S(1)} custom-call(f32[4096,256]{1,0:T(8,128)} %slab_ref.1, f32[512,512]{1,0:T(8,128)} %panel_ref.1, s32[512]{0:T(512)} %pivots_ref.1, s32[1,512]{1,0:T(1,128)} %bitcast.1, f32[512,512]{1,0:T(8,128)} %inv_lower_ref.1, f32[512,512]{1,0:T(8,128)} %inv_upper_ref.1), custom_call_target="tpu_custom_call" | custom-call | flops 3221225472 | bytes 8388608 | tf_op jit(solution)/shard_map/pallas_call | solution.py:474
  74.2 2.0 %copy.7 = f32[4096,256]{1,0:T(8,128)} copy(f32[4096,256]{1,0:T(8,128)S(1)} %shard_map.55) | data formatting | bytes 8388608

commit v6 on v5

--- a/solution.py
+++ b/solution.py
@@ -40,7 +40,7 @@
     guest, guest_split, direct, direct_landed,
     load_sem, link_send, link_recv, product_send, product_recv,
     pick_send, pick_recv, x_send, x_recv, half_send, half_recv, peer_send, peer_recv,
-    guest_send, guest_recv, direct_send, direct_recv,
+    detour, guest_send, guest_recv, direct_send, direct_recv, detour_send, detour_recv,
 ):
     slab = out_ref
     prow = lax.axis_index("prow")
@@ -49,8 +49,12 @@
     z, y = pcol // 2, pcol % 2
     rows, nb = panel_ref.shape
     unit = rows // 8
-    pieces = [(0, 2 * unit), (2 * unit, 2 * unit), (4 * unit, 2 * unit)]
-    pieces += [(6 * unit, unit), (7 * unit, unit)]
+    step_rows = rows // 16
+    pieces, edge = [], 0
+    for size in (4, 4, 3, 3, 2):
+        pieces.append((edge, size * step_rows))
+        edge += size * step_rows
+    groups = [(0, pieces[3][0]), (pieces[3][0], rows - pieces[3][0])]
     late = (3, 4)
     late_start = pieces[late[0]][0]
     late_span = pl.ds(late_start, rows - late_start)
@@ -127,7 +131,7 @@
         block = block_at(direction, distance)
         spot = raw.at[block, pl.ds(*pieces[g])]
         return remote(
-            spot, spot, link_send.at[direction * n_z + distance],
+            spot, spot, link_send.at[direction * (n_z - 1) + distance % (n_z - 1)],
             link_recv.at[(block - direction) * len(pieces) + g],
             right if direction == 0 else left,
         )
@@ -141,22 +145,17 @@
     panel_load.wait()
     n_peers = len(fixed) + has_left.astype(jnp.int32) + has_right.astype(jnp.int32)
     pl.semaphore_wait(barrier, n_peers)
-    def start_links():
-        for loaded in (True, False):
-            for direction in (0, 1):
-                near = (2 * z < n_z) if direction == 1 else (2 * z >= n_z)
-                for g in range(len(pieces)):
-                    @pl.when(goes(direction, g) & (near if loaded else ~near))
-                    def _():
-                        link(direction, 0, g).start()
-
-    pl.when(core == 0)(start_links)
+    for g in range(len(pieces)):
+        for direction in (0, 1):
+            @pl.when(goes(direction, g))
+            def _():
+                link(direction, 0, g).start()
+
     for i in range(3):
         peer_copy(i).start()
 
     pivot_load.wait()
     slab_load.wait()
-    pl.when(core != 0)(start_links)
 
     def pick(k, carry):
         local = pivots[k] - first_row
@@ -280,11 +279,26 @@
             guest_recv.at[direction], left if direction == 0 else right,
         )
 
-    def direct_copy(direction):
+    full = direct_landed.shape[0]
+    kept = full - detour.shape[0]
+    first = (x == 0) & (y == 0) & (n_x > 1)
+    helper = (x == 1) & (y == 0)
+
+    def direct_copy(direction, count):
         return remote(
-            direct.at[direction], direct_landed, direct_send.at[direction],
-            direct_recv, right if direction == 0 else left,
-        )
+            direct.at[direction, pl.ds(0, count)], direct_landed.at[pl.ds(0, count)],
+            direct_send.at[direction], direct_recv,
+            right if direction == 0 else left,
+        )
+
+    def detour_copy(leg):
+        source = direct.at[1, pl.ds(kept, full - kept)] if leg == 0 else detour
+        target = direct_landed.at[pl.ds(kept, full - kept)] if leg == 2 else detour
+        device = ({"prow": 2 + core}, left, {"prow": core})[leg]
+        return remote(source, target, detour_send, detour_recv, device)
+
+    def of_first(direction):
+        return first if direction == 1 else x < 0
 
     for direction in (0, 1):
         @pl.when(guest_of(direction))
@@ -297,7 +311,7 @@
         return remote(
             stage.at[block, span], landed.at[block, span],
             product_send.at[block - direction],
-            product_recv.at[(block - direction) * len(pieces) + g], peer,
+            product_recv.at[(block - direction) * 2 + g // 3], peer,
         )
 
     def subtract(block, side, start, count, product):
@@ -319,13 +333,17 @@
                 product_copy(direction, distance, g).start()
                 subtract(block, y, start, count, products[:, :columns])
 
-    def take(distance, g):
-        start, count = pieces[g]
-        for direction in (0, 1):
-            @pl.when(comes(direction, distance, g))
+    def take(distance, group):
+        start, count = groups[group]
+        for direction in (0, 1):
+            @pl.when(comes(direction, distance, 3 * group))
             def _():
                 block = block_at(direction, distance)
-                product_copy(direction, distance, g).wait_recv()
+                landing = landed.at[block, pl.ds(start, count)]
+                remote(
+                    landing, landing, product_send.at[block - direction],
+                    product_recv.at[(block - direction) * 2 + group], peer,
+                ).wait_recv()
                 subtract(
                     block, 1 - y, start, count, landed[block, pl.ds(start, count), :]
                 )
@@ -366,7 +384,25 @@
                     jnp.concatenate([lower[1, z, late_span, :], low], axis=0),
                     guest_split[0], guest_split[1],
                 )
-                direct_copy(direction).start()
+                if direction == 1:
+                    @pl.when(first)
+                    def _():
+                        detour_copy(0).start()
+
+                    @pl.when(helper)
+                    def _():
+                        detour_copy(0).wait_recv()
+                        detour_copy(1).start()
+
+    def start_direct():
+        for direction in (0, 1):
+            @pl.when(host_of(direction) & of_first(direction))
+            def _():
+                direct_copy(direction, kept).start()
+
+            @pl.when(host_of(direction) & ~of_first(direction))
+            def _():
+                direct_copy(direction, full).start()
 
     for g in range(early[1]):
         multiply(1, g)
@@ -376,15 +412,26 @@
         multiply(1, g)
         lax.fori_loop(2 * (g - early[1]), 2 * (g - early[1]) + 2, multiply_own, 0)
 
+    def pass_detour():
+        @pl.when(guest_of(1) & helper)
+        def _():
+            detour_copy(1).wait_recv()
+            detour_copy(2).start()
+
     def step(distance, final_step):
         for g in range(len(pieces)):
             prepare(distance, g)
             multiply(distance, g)
             if isinstance(distance, int) and not final_step and g < 4:
                 multiply_peer(g)
-            take(distance - 1, g)
-            if final_step and g >= 2:
-                take(distance, g - 2)
+            if isinstance(distance, int) and not final_step and g == 3:
+                serve()
+            if g in (2, 4):
+                take(distance - 1, g // 4)
+            if final_step and g == 3:
+                pass_detour()
+            if final_step and g == 4:
+                take(distance, 0)
 
     if n_z <= 3:
         for i in range(4):
@@ -392,9 +439,13 @@
     if n_z > 3:
         step(2, False)
         lax.fori_loop(3, n_z - 1, lambda d, c: (step(d, False), c)[1], 0)
-    serve()
+    if n_z <= 3:
+        serve()
+    start_direct()
     if n_z > 2:
         step(n_z - 1, True)
+    else:
+        pass_detour()
 
     def settle_products(direction, distance):
         block = block_at(direction, distance)
@@ -417,7 +468,7 @@
         def wait(count):
             spot = raw.at[block, pl.ds(0, count)]
             remote(
-                spot, spot, link_send.at[direction * n_z + distance], link_recv.at[0],
+                spot, spot, link_send.at[direction * (n_z - 1) + distance % (n_z - 1)], link_recv.at[0],
                 right if direction == 0 else left,
             ).wait_send()
 
@@ -437,8 +488,8 @@
         @pl.when(guest_of(direction))
         def _():
             guest_copy(direction).wait_send()
-    for g in range(3 if n_z > 2 else 0, len(pieces)):
-        take(n_z - 1, g)
+    for group in range(1 if n_z > 2 else 0, 2):
+        take(n_z - 1, group)
 
     def settle_late(distance, carry):
         for direction in (0, 1):
@@ -449,11 +500,36 @@
     for direction in (0, 1):
         @pl.when(host_of(direction))
         def _():
-            direct_copy(direction).wait_send()
+            @pl.when(of_first(direction))
+            def _():
+                direct_copy(direction, kept).wait_send()
+                detour_copy(0).wait_send()
+
+            @pl.when(~of_first(direction))
+            def _():
+                direct_copy(direction, full).wait_send()
+
+            if direction == 1:
+                @pl.when(helper)
+                def _():
+                    detour_copy(1).wait_send()
 
         @pl.when(guest_of(direction))
         def _():
-            direct_copy(direction).wait_recv()
+            @pl.when(of_first(direction))
+            def _():
+                direct_copy(direction, kept).wait_recv()
+                detour_copy(2).wait_recv()
+
+            @pl.when(~of_first(direction))
+            def _():
+                direct_copy(direction, full).wait_recv()
+
+            if direction == 1:
+                @pl.when(helper)
+                def _():
+                    detour_copy(2).wait_send()
+
             count = rows - late_start
             block = block_at(direction, 1)
             subtract(block, y, late_start, count, direct_landed[:count])
@@ -467,7 +543,7 @@
     def local(slab, panel, pivots, inv_lower, inv_upper):
         (row_count, columns), (rows, nb) = slab.shape, panel.shape
         half = columns // 2
-        pair = rows // 2
+        pair = rows * 5 // 8
         hbm = pl.BlockSpec(memory_space=pltpu.HBM)
         dma = pltpu.SemaphoreType.DMA
         flops = 2 * row_count * nb * (nb + columns)
@@ -506,10 +582,10 @@
                 pltpu.VMEM((2, pair, columns), F32),
                 pltpu.VMEM((pair, columns), F32),
                 dma((6,)),
-                dma((2 * n_z,)),
+                dma((2 * (n_z - 1),)),
                 dma((n_pieces * (n_z - 1),)),
                 dma((n_z - 1,)),
-                dma((n_pieces * (n_z - 1),)),
+                dma((2 * (n_z - 1),)),
                 dma,
                 dma,
                 dma((max(n_x - 1, 1),)),
@@ -518,9 +594,12 @@
                 dma((3,)),
                 dma,
                 dma((5,)),
+                pltpu.VMEM((max(rows // 16, 8), columns), F32),
                 dma((2,)),
                 dma((2,)),
                 dma((2,)),
+                dma,
+                dma,
                 dma,
             ],
             compiler_params=pltpu.CompilerParams(

time: 76.3 us -> 74.5 us (0.976)
  Pallas kernels: 74.1 us -> 72.3 us
    pallas_call x1, Pallas kernels: 74.1 us -> 72.3 us  [local(): pl.pallas_call(functools.partial(kernel, n_x, n_z, early), out_shape=pltp...]
where the time goes in v6:
time: 74.5 us; the launch traced here: 74.3 us
  Pallas kernels  72.3 us (97%)
  local copies, waits for them, and re-layouts  2.02 us (3%)
    pallas_call x1, Pallas kernels, local(): pl.pallas_call(functools.partial(kernel, n_x, n_z, early), out_shape=pltp...  72.3 us
    unnamed x1, local copies, waits for them, and re-layouts  2.02 us

profile of v6, /device:TPU:0, one launch (start us, length us, event | category | flops | bytes accessed | tf_op | source)
XLA Modules:
  0.0 74.3 jit_solution(9493116391983300415)
XLA Ops:
  0.0 72.3 %shard_map.55 = f32[4096,256]{1,0:T(8,128)S(1)} custom-call(f32[4096,256]{1,0:T(8,128)} %slab_ref.1, f32[512,512]{1,0:T(8,128)} %panel_ref.1, s32[512]{0:T(512)} %pivots_ref.1, s32[1,512]{1,0:T(1,128)} %bitcast.1, f32[512,512]{1,0:T(8,128)} %inv_lower_ref.1, f32[512,512]{1,0:T(8,128)} %inv_upper_ref.1), custom_call_target="tpu_custom_call" | custom-call | flops 3221225472 | bytes 8388608 | tf_op jit(solution)/shard_map/pallas_call | solution.py:550
  72.3 2.0 %copy.7 = f32[4096,256]{1,0:T(8,128)} copy(f32[4096,256]{1,0:T(8,128)S(1)} %shard_map.55) | data formatting | bytes 8388608

commit v7 on v6

--- a/solution.py
+++ b/solution.py
@@ -40,7 +40,7 @@
     guest, guest_split, direct, direct_landed,
     load_sem, link_send, link_recv, product_send, product_recv,
     pick_send, pick_recv, x_send, x_recv, half_send, half_recv, peer_send, peer_recv,
-    detour, guest_send, guest_recv, direct_send, direct_recv, detour_send, detour_recv,
+    detour, bridge, bridge_send, bridge_recv, onward_recv, guest_send, guest_recv, direct_send, direct_recv, detour_send, detour_recv,
 ):
     slab = out_ref
     prow = lax.axis_index("prow")
@@ -284,12 +284,32 @@
     first = (x == 0) & (y == 0) & (n_x > 1)
     helper = (x == 1) & (y == 0)
 
-    def direct_copy(direction, count):
+    moved = bridge.shape[1]
+
+    def direct_copy(direction, count, start):
+        span = pl.ds(start, count - start)
         return remote(
-            direct.at[direction, pl.ds(0, count)], direct_landed.at[pl.ds(0, count)],
+            direct.at[direction, span], direct_landed.at[span],
             direct_send.at[direction], direct_recv,
             right if direction == 0 else left,
         )
+
+    def bridge_copy(direction):
+        return remote(
+            direct.at[direction, pl.ds(0, moved)], bridge.at[direction],
+            bridge_send.at[direction], bridge_recv.at[direction], partner,
+        )
+
+    def bridge_onward(direction):
+        column = right if direction == 0 else left
+        return remote(
+            bridge.at[direction], direct_landed.at[pl.ds(0, moved)],
+            bridge_send.at[direction], onward_recv, {**partner, **column},
+        )
+
+    def by_core(action, direction, count):
+        pl.when(core == 0)(lambda: getattr(direct_copy(direction, count, moved), action)())
+        pl.when(core != 0)(lambda: getattr(direct_copy(direction, count, 0), action)())
 
     def detour_copy(leg):
         source = direct.at[1, pl.ds(kept, full - kept)] if leg == 0 else detour
@@ -396,13 +416,22 @@
 
     def start_direct():
         for direction in (0, 1):
+            @pl.when(host_of(direction) & (core == 0))
+            def _():
+                bridge_copy(direction).start()
+
+            @pl.when(host_of(direction) & (core != 0))
+            def _():
+                bridge_copy(direction).wait_recv()
+                bridge_onward(direction).start()
+
             @pl.when(host_of(direction) & of_first(direction))
             def _():
-                direct_copy(direction, kept).start()
+                by_core("start", direction, kept)
 
             @pl.when(host_of(direction) & ~of_first(direction))
             def _():
-                direct_copy(direction, full).start()
+                by_core("start", direction, full)
 
     for g in range(early[1]):
         multiply(1, g)
@@ -496,18 +525,22 @@
             settle_products(direction, distance)
         return carry
 
+    for direction in (0, 1):
+        pl.when(host_of(direction) & (core == 0))(lambda: bridge_copy(direction).wait_send())
+        pl.when(host_of(direction) & (core != 0))(lambda: bridge_onward(direction).wait_send())
+
     lax.fori_loop(1, n_z, settle_late, 0)
     for direction in (0, 1):
         @pl.when(host_of(direction))
         def _():
             @pl.when(of_first(direction))
             def _():
-                direct_copy(direction, kept).wait_send()
+                by_core("wait_send", direction, kept)
                 detour_copy(0).wait_send()
 
             @pl.when(~of_first(direction))
             def _():
-                direct_copy(direction, full).wait_send()
+                by_core("wait_send", direction, full)
 
             if direction == 1:
                 @pl.when(helper)
@@ -518,18 +551,19 @@
         def _():
             @pl.when(of_first(direction))
             def _():
-                direct_copy(direction, kept).wait_recv()
+                by_core("wait_recv", direction, kept)
                 detour_copy(2).wait_recv()
 
             @pl.when(~of_first(direction))
             def _():
-                direct_copy(direction, full).wait_recv()
+                by_core("wait_recv", direction, full)
 
             if direction == 1:
                 @pl.when(helper)
                 def _():
                     detour_copy(2).wait_send()
 
+            pl.when(core == 0)(lambda: bridge_onward(direction).wait_recv())
             count = rows - late_start
             block = block_at(direction, 1)
             subtract(block, y, late_start, count, direct_landed[:count])
@@ -595,6 +629,10 @@
                 dma,
                 dma((5,)),
                 pltpu.VMEM((max(rows // 16, 8), columns), F32),
+                pltpu.VMEM((2, rows // 8, columns), F32),
+                dma((2,)),
+                dma((2,)),
+                dma,
                 dma((2,)),
                 dma((2,)),
                 dma((2,)),

time: 74.5 us -> 74.5 us (level)
  no operation moved by 1% of the time
where the time goes in v7:
time: 74.5 us; the launch traced here: 74.1 us
  Pallas kernels  72.1 us (97%)
  local copies, waits for them, and re-layouts  2.02 us (3%)
    pallas_call x1, Pallas kernels, local(): pl.pallas_call(functools.partial(kernel, n_x, n_z, early), out_shape=pltp...  72.1 us
    unnamed x1, local copies, waits for them, and re-layouts  2.02 us

profile of v7, /device:TPU:0, one launch (start us, length us, event | category | flops | bytes accessed | tf_op | source)
XLA Modules:
  0.0 74.1 jit_solution(1994877188025393376)
XLA Ops:
  0.0 72.1 %shard_map.55 = f32[4096,256]{1,0:T(8,128)S(1)} custom-call(f32[4096,256]{1,0:T(8,128)} %slab_ref.1, f32[512,512]{1,0:T(8,128)} %panel_ref.1, s32[512]{0:T(512)} %pivots_ref.1, s32[1,512]{1,0:T(1,128)} %bitcast.1, f32[512,512]{1,0:T(8,128)} %inv_lower_ref.1, f32[512,512]{1,0:T(8,128)} %inv_upper_ref.1), custom_call_target="tpu_custom_call" | custom-call | flops 3221225472 | bytes 8388608 | tf_op jit(solution)/shard_map/pallas_call | solution.py:584
  72.1 2.0 %copy.7 = f32[4096,256]{1,0:T(8,128)} copy(f32[4096,256]{1,0:T(8,128)S(1)} %shard_map.55) | data formatting | bytes 8388608

commit v8 on v7

--- a/solution.py
+++ b/solution.py
@@ -143,6 +143,7 @@
         )
 
     panel_load.wait()
+    slots = guest_send.shape[0]
     n_peers = len(fixed) + has_left.astype(jnp.int32) + has_right.astype(jnp.int32)
     pl.semaphore_wait(barrier, n_peers)
     for g in range(len(pieces)):
@@ -275,8 +276,8 @@
 
     def guest_copy(direction):
         return remote(
-            halves.at[0:2], guest.at[direction], guest_send.at[direction],
-            guest_recv.at[direction], left if direction == 0 else right,
+            halves.at[0:2], guest.at[direction], guest_send.at[direction % slots],
+            guest_recv.at[direction % slots], left if direction == 0 else right,
         )
 
     full = direct_landed.shape[0]
@@ -290,21 +291,21 @@
         span = pl.ds(start, count - start)
         return remote(
             direct.at[direction, span], direct_landed.at[span],
-            direct_send.at[direction], direct_recv,
+            direct_send.at[direction % slots], direct_recv,
             right if direction == 0 else left,
         )
 
     def bridge_copy(direction):
         return remote(
             direct.at[direction, pl.ds(0, moved)], bridge.at[direction],
-            bridge_send.at[direction], bridge_recv.at[direction], partner,
+            bridge_send.at[direction % slots], bridge_recv.at[direction % slots], partner,
         )
 
     def bridge_onward(direction):
         column = right if direction == 0 else left
         return remote(
             bridge.at[direction], direct_landed.at[pl.ds(0, moved)],
-            bridge_send.at[direction], onward_recv, {**partner, **column},
+            bridge_send.at[direction % slots], onward_recv, {**partner, **column},
         )
 
     def by_core(action, direction, count):
@@ -630,12 +631,12 @@
                 dma((5,)),
                 pltpu.VMEM((max(rows // 16, 8), columns), F32),
                 pltpu.VMEM((2, rows // 8, columns), F32),
-                dma((2,)),
-                dma((2,)),
+                dma((1 if n_z > 3 else 2,)),
+                dma((1 if n_z > 3 else 2,)),
                 dma,
-                dma((2,)),
-                dma((2,)),
-                dma((2,)),
+                dma((1 if n_z > 3 else 2,)),
+                dma((1 if n_z > 3 else 2,)),
+                dma((1 if n_z > 3 else 2,)),
                 dma,
                 dma,
                 dma,

time: 74.5 us -> 74.4 us (level)
  no operation moved by 1% of the time
where the time goes in v8:
time: 74.4 us; the launch traced here: 74.1 us
  Pallas kernels  72 us (97%)
  local copies, waits for them, and re-layouts  2.02 us (3%)
    pallas_call x1, Pallas kernels, local(): pl.pallas_call(functools.partial(kernel, n_x, n_z, early), out_shape=pltp...  72 us
    unnamed x1, local copies, waits for them, and re-layouts  2.02 us

profile of v8, /device:TPU:0, one launch (start us, length us, event | category | flops | bytes accessed | tf_op | source)
XLA Modules:
  0.0 74.1 jit_solution(10628686516659302662)
XLA Ops:
  0.0 72.0 %shard_map.55 = f32[4096,256]{1,0:T(8,128)S(1)} custom-call(f32[4096,256]{1,0:T(8,128)} %slab_ref.1, f32[512,512]{1,0:T(8,128)} %panel_ref.1, s32[512]{0:T(512)} %pivots_ref.1, s32[1,512]{1,0:T(1,128)} %bitcast.1, f32[512,512]{1,0:T(8,128)} %inv_lower_ref.1, f32[512,512]{1,0:T(8,128)} %inv_upper_ref.1), custom_call_target="tpu_custom_call" | custom-call | flops 3221225472 | bytes 8388608 | tf_op jit(solution)/shard_map/pallas_call | solution.py:585
  72.1 2.0 %copy.7 = f32[4096,256]{1,0:T(8,128)} copy(f32[4096,256]{1,0:T(8,128)S(1)} %shard_map.55) | data formatting | bytes 8388608
